TPU v7x, 32 devices: a whole 2x2x4 slice. The times are simulated.
32 devices in a mesh: lat: 4 (over y, x), lon: 4 (over z), ens: 2 (over core).
Axes of the slice: x: 2, y: 2, z: 4, core: 2. Of those that a mesh axis runs over, the one named last changes fastest.
Arguments:
- parameters: float32 [2, 128, 32, 512], P(None, 'ens', 'lat', 'lon'), may hold values from -1.2 to 1.2, as said below
- initial_height: float32 [32, 512], P('lat', 'lon'), may hold values from -6 to 6
- initial_speed: float32 [2, 32, 512], P(None, 'lat', 'lon'), may hold values from -4 to 4
- obs_slots: int32 [2, 16, 16, 8], P(None, ('lat', 'lon')), may hold values from -1 to 1023, as said below
- obs_values: float32 [2, 16, 16, 8], P(None, ('lat', 'lon')), may hold values from -6 to 6
- obs_precision: float32 [2, 16, 16, 8], P(None, ('lat', 'lon')), may hold values from 0 to 2, as said below
Outputs:
- calibrated: float32 [2, 128, 32, 512], P(None, 'ens', 'lat', 'lon')
Inputs may be any that keep to these rules, and one draw needn't show every extreme that they name: `obs_slots`: for each iteration and owner, the live slots towards one receiver come first and name distinct cells of the owner's block (local index row * 128 + column); no cell is named twice by one owner in one iteration; in each iteration some receiving block has all 8 slots live from every owner. `obs_precision`: zero exactly where the matching slot of obs_slots (with receiver and owner swapped) is empty, 0.5 or more elsewhere. `parameters`: friction rates lie in 0.02 to 0.2, forcing in -1.2 to 1.2.
All inputs are finite; a program needn't handle non-finite values.
Results may differ from a plain program's by a relative error of at most 0.0003.
Values sent between devices are 32-bit elements; how exact they have to be, the bound alone decides.
A program may use at most 64 MiB of HBM per device.

v0:
```python
import math
import jax
import jax.numpy as jnp
from jax import lax
from jax.sharding import PartitionSpec as P

STEPS = 6
ITERS = 2
depth_step = 0.7
gravity_step = 0.7
coriolis = 0.1


def padded_2(value, sides, width, wrap):
    for axis, dim in sides:
        peers, length = (lax.axis_size(axis), value.shape[dim])
        up = [(i, (i + 1) % peers) for i in range(peers if wrap else peers - 1)]
        down = [(j, i) for i, j in up]
        last = lax.slice_in_dim(value, length - width, length, axis=dim)
        leading = lax.slice_in_dim(value, 0, width, axis=dim)
        before = lax.ppermute(last, axis, up)
        after = lax.ppermute(leading, axis, down)
        value = jnp.concatenate([before, value, after], axis=dim)
    return value


def wall_rows(padded):
    row_count = padded.shape[-2]
    position = lax.axis_index("lat")
    last_block = lax.axis_size("lat") - 1
    row_ids = lax.broadcasted_iota(jnp.int32, (row_count, 1), 0)
    lower_wall = jnp.logical_and(row_ids == 0, position == 0)
    upper_wall = jnp.logical_and(row_ids == row_count - 1, position == last_block)
    keep_rows = jnp.logical_not(jnp.logical_or(lower_wall, upper_wall))
    return padded * keep_rows.astype(padded.dtype)


def advance(height, speeds, friction, forcing):
    east_padded = padded_2(speeds[0], (("lon", 2),), 1, True)
    north_padded = padded_2(speeds[1], (("lat", 1),), 1, False)
    east_diff = east_padded[:, :, 2:] - east_padded[:, :, :-2]
    north_diff = north_padded[:, 2:, :] - north_padded[:, :-2, :]
    height = height - depth_step * (east_diff + north_diff) + forcing
    padded_height = padded_2(height, (("lat", 1), ("lon", 2)), 1, True)
    padded_height = wall_rows(padded_height)
    slope_east = padded_height[:, 1:-1, 2:] - padded_height[:, 1:-1, :-2]
    slope_north = padded_height[:, 2:, 1:-1] - padded_height[:, :-2, 1:-1]
    eastward = (1.0 - friction) * speeds[0] - gravity_step * slope_east + coriolis * speeds[1]
    northward = (1.0 - friction) * speeds[1] - gravity_step * slope_north - coriolis * speeds[0]
    return (height, jnp.stack([eastward, northward]))


def forward(parameters, initial_height, initial_speed):
    members = parameters.shape[1]
    height = jnp.broadcast_to(initial_height, (members,) + initial_height.shape)
    speeds = jnp.broadcast_to(initial_speed[:, None], (2, members) + initial_height.shape)
    for substep in range(STEPS):
        height, speeds = advance(height, speeds, parameters[0], parameters[1])
    return height


def predict(height, cells):
    flattened = height.reshape(height.shape[0], -1)
    wanted = cells.reshape(-1)
    picked = jnp.take(flattened, jnp.clip(wanted, 0, flattened.shape[1] - 1), axis=1)
    picked = jnp.where(wanted[None, :] >= 0, picked, jnp.float32(0.0))
    return picked.T.reshape(cells.shape[0], -1)


def gram_terms(predicted, observed, precision):
    members = predicted.shape[1]
    centre = jnp.mean(predicted, axis=1, keepdims=True)
    spread = predicted - centre
    weighted = spread * precision[:, None]
    misfit = observed[:, None] - predicted
    gram_part = jnp.dot(spread.T, weighted, precision=lax.Precision.HIGHEST) / members
    cross_part = jnp.dot(weighted.T, misfit, precision=lax.Precision.HIGHEST) / math.sqrt(members)
    return (gram_part, cross_part)


def solve_weights(gram_part, cross_part):
    members = gram_part.shape[0]
    system = jnp.eye(members, dtype=jnp.float32) + gram_part
    factor = jnp.linalg.cholesky(system)
    weights = jax.scipy.linalg.cho_solve((factor, True), cross_part) / math.sqrt(members)
    return weights - jnp.mean(weights, axis=0, keepdims=True)


def per_device(parameters, initial_height, initial_speed, obs_slots, obs_values, obs_precision):
    owners = obs_slots.shape[2]
    slot_count = obs_slots.shape[3]
    members_here = parameters.shape[1]
    member_block = lax.axis_index("ens")
    owner_values, owner_precision = (
        lax.all_to_all(obs_values[:, 0], ("lat", "lon"), split_axis=1, concat_axis=1, tiled=True),
        lax.all_to_all(
            obs_precision[:, 0], ("lat", "lon"), split_axis=1, concat_axis=1, tiled=True
        ),
    )
    for iteration in range(ITERS):
        height = forward(parameters, initial_height, initial_speed)
        outgoing = predict(height, obs_slots[iteration, 0])
        received = outgoing
        observed = owner_values[iteration]
        precision = owner_precision[iteration]
        received = received.reshape(owners, slot_count, members_here)
        gathered = lax.all_gather(received, "ens", axis=2, tiled=True)
        members = gathered.shape[2]
        gram_part, cross_part = gram_terms(
            gathered.reshape(-1, members), observed.reshape(-1), precision.reshape(-1)
        )
        gram_part, cross_part = lax.psum((gram_part, cross_part), ("lat", "lon"))
        centred = solve_weights(gram_part, cross_part)
        local_weights = lax.dynamic_slice_in_dim(
            centred, member_block * members_here, members_here, 1
        )
        starting = jnp.zeros(
            (2, members_here, parameters.shape[2] * parameters.shape[3]), jnp.float32
        )
        pieces = lax.all_gather(parameters, "ens", axis=1, tiled=True)
        stacked = pieces.reshape(pieces.shape[0], pieces.shape[1], -1)
        increment = starting + jnp.einsum(
            "pjc,jm->pmc", stacked, local_weights, precision=lax.Precision.HIGHEST
        )
        parameters = parameters + increment.reshape(parameters.shape)
    return parameters


def solution(mesh):
    placed = (
        P(None, "ens", "lat", "lon"),
        P("lat", "lon"),
        P(None, "lat", "lon"),
        P(None, ("lat", "lon"), None, None),
        P(None, ("lat", "lon"), None, None),
        P(None, ("lat", "lon"), None, None),
    )
    return jax.shard_map(
        per_device,
        mesh=mesh,
        in_specs=placed,
        out_specs=P(None, "ens", "lat", "lon"),
        check_vma=False,
    )
```

profile of v0, /device:TPU:0, one launch (start us, length us, event | category | flops | bytes accessed | tf_op | source)
XLA Modules:
  0.0 800.0 jit_solution(9738654765726643208)
XLA Ops:
  9.5 5.5 collective-permute-start.3
  15.3 4.2 collective-permute-start
  19.6 6.5 collective-permute-done
  26.2 4.8 collective-permute-done.1
  42.6 12.8 %collective-permute-done.6 = f32[64,10,1]{2,1,0:T(8,128)S(1)} collective-permute-done((f32[64,10,1]{2,1,0:T(8,128)S(1)}, f32[64,10,1]{2,1,0:T(8,128)S(1)}, u32[]{:S(2)}, u32[]{:S(2)}) %collective-permute-start.6) | collective-permute-done | bytes 2592 | tf_op jit(solution)/shard_map/ppermute | solution.py:21
  55.4 6.8 collective-permute-done.7
  64.6 4.5 collective-permute-start.11
  71.5 10.8 %collective-permute-done.8 = f32[64,8,1]{2,1,0:T(8,128)S(1)} collective-permute-done((f32[64,8,1]{2,1,0:T(8,128)S(1)}, f32[64,8,1]{2,1,0:T(8,128)S(1)}, u32[]{:S(2)}, u32[]{:S(2)}) %collective-permute-start.8) | collective-permute-done | bytes 2080 | tf_op jit(solution)/shard_map/ppermute | solution.py:22
  90.0 3.5 collective-permute-start.15
  93.5 12.5 %collective-permute-done.14 = f32[64,10,1]{2,1,0:T(8,128)S(1)} collective-permute-done((f32[64,10,1]{2,1,0:T(8,128)S(1)}, f32[64,10,1]{2,1,0:T(8,128)S(1)}, u32[]{:S(2)}, u32[]{:S(2)}) %collective-permute-start.14) | collective-permute-done | bytes 2592 | tf_op jit(solution)/shard_map/ppermute | solution.py:21
  106.0 5.6 collective-permute-done.15
  114.0 4.5 collective-permute-start.19
  118.7 3.0 collective-permute-start.16
  121.7 10.4 %collective-permute-done.16 = f32[64,8,1]{2,1,0:T(8,128)S(1)} collective-permute-done((f32[64,8,1]{2,1,0:T(8,128)S(1)}, f32[64,8,1]{2,1,0:T(8,128)S(1)}, u32[]{:S(2)}, u32[]{:S(2)}) %collective-permute-start.16) | collective-permute-done | bytes 2080 | tf_op jit(solution)/shard_map/ppermute | solution.py:22
  140.3 3.3 collective-permute-start.23
  144.3 4.1 all-to-all-start.1
  148.4 7.9 collective-permute-done.22
  156.3 5.7 collective-permute-done.23
  164.3 2.9 collective-permute-start.24
  168.5 4.5 collective-permute-start.27
  173.1 5.0 collective-permute-done.24
  184.9 3.2 collective-permute-start.31
  188.6 12.2 %collective-permute-done.30 = f32[64,10,1]{2,1,0:T(8,128)S(1)} collective-permute-done((f32[64,10,1]{2,1,0:T(8,128)S(1)}, f32[64,10,1]{2,1,0:T(8,128)S(1)}, u32[]{:S(2)}, u32[]{:S(2)}) %collective-permute-start.30) | collective-permute-done | bytes 2592 | tf_op jit(solution)/shard_map/ppermute | solution.py:21
  200.8 6.1 collective-permute-done.31
  211.7 4.5 collective-permute-start.35
  216.2 5.8 collective-permute-done.32
  230.0 3.3 collective-permute-start.39
  233.2 4.1 all-to-all-start
  238.8 7.4 collective-permute-done.38
  246.2 6.6 collective-permute-done.39
  259.1 5.2 collective-permute-start.43
  265.7 3.2 collective-permute-done.40
  277.9 104.7 %all-reduce.7.cloned.1.call-done = (f32[128,128]{1,0:T(8,128)}, f32[128,128]{0,1:T(8,128)}) async-done(((f32[128,128]{1,0:T(8,128)}, f32[128,128]{0,1:T(8,128)}), (f32[128,128]{1,0:T(8,128)}, f32[128,128]{0,1:T(8,128)})) %all-reduce.7.cloned.1.call-update) | async-done | bytes 131088 | tf_op jit(solution)/shard_map/psum | solution.py:112
  384.2 11.7 %cholesky.44 = f32[128,128]{1,0:T(8,128)S(1)} custom-call(f32[128,128]{1,0:T(8,128)S(1)} %fusion.151), custom_call_target="Cholesky" | custom-call | tf_op jit(solution)/shard_map/jit(cholesky)/cholesky | solution.py:84
  397.3 9.8 %custom-call.8 = f32[1,128,128]{1,2,0:T(8,128)S(1)} custom-call(f32[1,128,128]{2,1,0:T(8,128)S(1)} %fusion.135), custom_call_target="InvertDiagBlocksLowerTriangular" | custom-call | tf_op jit(solution)/shard_map/jit(_cho_solve)/triangular_solve | solution.py:85
  417.9 3.1 collective-permute-start.47
  420.9 12.8 %collective-permute-done.46 = f32[64,10,1]{2,1,0:T(8,128)S(1)} collective-permute-done((f32[64,10,1]{2,1,0:T(8,128)S(1)}, f32[64,10,1]{2,1,0:T(8,128)S(1)}, u32[]{:S(2)}, u32[]{:S(2)}) %collective-permute-start.46) | collective-permute-done | bytes 2592 | tf_op jit(solution)/shard_map/ppermute | solution.py:21
  433.7 5.6 collective-permute-done.47
  441.7 4.8 collective-permute-start.51
  448.8 10.4 %collective-permute-done.48 = f32[64,8,1]{2,1,0:T(8,128)S(1)} collective-permute-done((f32[64,8,1]{2,1,0:T(8,128)S(1)}, f32[64,8,1]{2,1,0:T(8,128)S(1)}, u32[]{:S(2)}, u32[]{:S(2)}) %collective-permute-start.48) | collective-permute-done | bytes 2080 | tf_op jit(solution)/shard_map/ppermute | solution.py:22
  470.8 12.6 %collective-permute-done.54 = f32[64,10,1]{2,1,0:T(8,128)S(1)} collective-permute-done((f32[64,10,1]{2,1,0:T(8,128)S(1)}, f32[64,10,1]{2,1,0:T(8,128)S(1)}, u32[]{:S(2)}, u32[]{:S(2)}) %collective-permute-start.54) | collective-permute-done | bytes 2592 | tf_op jit(solution)/shard_map/ppermute | solution.py:21
  483.3 6.4 collective-permute-done.55
  492.1 4.5 collective-permute-start.59
  499.4 7.2 collective-permute-done.56
  506.6 3.5 collective-permute-done.57
  520.5 12.8 %collective-permute-done.62 = f32[64,10,1]{2,1,0:T(8,128)S(1)} collective-permute-done((f32[64,10,1]{2,1,0:T(8,128)S(1)}, f32[64,10,1]{2,1,0:T(8,128)S(1)}, u32[]{:S(2)}, u32[]{:S(2)}) %collective-permute-start.62) | collective-permute-done | bytes 2592 | tf_op jit(solution)/shard_map/ppermute | solution.py:21
  533.2 6.3 collective-permute-done.63
  541.9 4.5 collective-permute-start.67
  546.6 2.8 collective-permute-start.64
  549.4 7.2 collective-permute-done.64
  556.6 3.5 collective-permute-done.65
  570.5 12.8 %collective-permute-done.70 = f32[64,10,1]{2,1,0:T(8,128)S(1)} collective-permute-done((f32[64,10,1]{2,1,0:T(8,128)S(1)}, f32[64,10,1]{2,1,0:T(8,128)S(1)}, u32[]{:S(2)}, u32[]{:S(2)}) %collective-permute-start.70) | collective-permute-done | bytes 2592 | tf_op jit(solution)/shard_map/ppermute | solution.py:21
  583.3 4.5 collective-permute-done.71
  590.3 4.5 collective-permute-start.75
  595.0 2.8 collective-permute-start.72
  597.8 7.4 collective-permute-done.72
  605.2 3.1 collective-permute-done.73
  618.9 12.1 %collective-permute-done.78 = f32[64,10,1]{2,1,0:T(8,128)S(1)} collective-permute-done((f32[64,10,1]{2,1,0:T(8,128)S(1)}, f32[64,10,1]{2,1,0:T(8,128)S(1)}, u32[]{:S(2)}, u32[]{:S(2)}) %collective-permute-start.78) | collective-permute-done | bytes 2592 | tf_op jit(solution)/shard_map/ppermute | solution.py:21
  631.0 4.3 collective-permute-done.79
  640.1 4.5 collective-permute-start.83
  646.7 3.0 collective-permute-done.81
  657.6 105.3 %all-reduce.5.cloned.1.call-done = (f32[128,128]{1,0:T(8,128)}, f32[128,128]{0,1:T(8,128)}) async-done(((f32[128,128]{1,0:T(8,128)}, f32[128,128]{0,1:T(8,128)}), (f32[128,128]{1,0:T(8,128)}, f32[128,128]{0,1:T(8,128)})) %all-reduce.5.cloned.1.call-update) | async-done | bytes 131088 | tf_op jit(solution)/shard_map/psum | solution.py:112
  764.6 11.7 %cholesky.55 = f32[128,128]{1,0:T(8,128)S(1)} custom-call(f32[128,128]{1,0:T(8,128)S(1)} %fusion.146), custom_call_target="Cholesky" | custom-call | tf_op jit(solution)/shard_map/jit(cholesky)/cholesky | solution.py:84
  777.7 9.8 %custom-call.9 = f32[1,128,128]{1,2,0:T(8,128)S(1)} custom-call(f32[1,128,128]{2,1,0:T(8,128)S(1)} %fusion.136), custom_call_target="InvertDiagBlocksLowerTriangular" | custom-call | tf_op jit(solution)/shard_map/jit(_cho_solve)/triangular_solve | solution.py:85
  (344 shorter events, 173.1 us)
Async XLA Ops:
  8.2 22.9 %collective-permute-start.2 = (f32[64,1,128]{2,1,0:T(1,128)S(1)}, f32[64,1,128]{2,1,0:T(1,128)S(1)}, u32[]{:S(2)}, u32[]{:S(2)}) collective-permute-start(f32[64,1,128]{2,1,0:T(1,128)S(1)} %broadcast_in_dim.82), channel_id=1, source_target_pairs={{8,0},{16,8},{24,16},{9,1},{17,9},{25,17},{10,2},{18,10},{26,18},{... | collective-permute-start | bytes 98312 | tf_op jit(solution)/shard_map/ppermute | solution.py:22
  9.5 21.5 %collective-permute-start.3 = (f32[64,1,128]{2,1,0:T(1,128)S(1)}, f32[64,1,128]{2,1,0:T(1,128)S(1)}, u32[]{:S(2)}, u32[]{:S(2)}) collective-permute-start(f32[64,1,128]{2,1,0:T(1,128)S(1)} %broadcast_in_dim.83), channel_id=1, source_target_pairs={{0,8},{8,16},{16,24},{1,9},{9,17},{17,25},{2,10},{10,18},{18,26},{... | collective-permute-start | bytes 98312 | tf_op jit(solution)/shard_map/ppermute | solution.py:21
  15.3 10.9 %collective-permute-start = (f32[64,8,1]{2,1,0:T(8,128)S(1)}, f32[64,8,1]{2,1,0:T(8,128)S(1)}, u32[]{:S(2)}, u32[]{:S(2)}) collective-permute-start(f32[64,8,1]{2,1,0:T(8,128)S(1)} %broadcast_in_dim.78), channel_id=1, source_target_pairs={{2,0},{4,2},{6,4},{0,6},{3,1},{5,3},{7,5},{1,7},{10,8},{12,10},{14... | collective-permute-start | bytes 6152 | tf_op jit(solution)/shard_map/ppermute | solution.py:22
  19.6 11.4 %collective-permute-start.1 = (f32[64,8,1]{2,1,0:T(8,128)S(1)}, f32[64,8,1]{2,1,0:T(8,128)S(1)}, u32[]{:S(2)}, u32[]{:S(2)}) collective-permute-start(f32[64,8,1]{2,1,0:T(8,128)S(1)} %broadcast_in_dim.79), channel_id=1, source_target_pairs={{0,2},{2,4},{4,6},{6,0},{1,3},{3,5},{5,7},{7,1},{8,10},{10,12},{12... | collective-permute-start | bytes 6152 | tf_op jit(solution)/shard_map/ppermute | solution.py:21
  38.7 16.6 %collective-permute-start.6 = (f32[64,10,1]{2,1,0:T(8,128)S(1)}, f32[64,10,1]{2,1,0:T(8,128)S(1)}, u32[]{:S(2)}, u32[]{:S(2)}) collective-permute-start(f32[64,10,1]{2,1,0:T(8,128)S(1)} %get-tuple-element.56), channel_id=1, source_target_pairs={{0,2},{2,4},{4,6},{6,0},{1,3},{3,5},{5,7},{7,1},{8,10},{10,12},{12... | collective-permute-start | bytes 7688 | tf_op jit(solution)/shard_map/ppermute | solution.py:21
  40.4 21.8 %collective-permute-start.7 = (f32[64,10,1]{2,1,0:T(8,128)S(1)}, f32[64,10,1]{2,1,0:T(8,128)S(1)}, u32[]{:S(2)}, u32[]{:S(2)}) collective-permute-start(f32[64,10,1]{2,1,0:T(8,128)S(1)} %get-tuple-element.57), channel_id=1, source_target_pairs={{2,0},{4,2},{6,4},{0,6},{3,1},{5,3},{7,5},{1,7},{10,8},{12,10},{14... | collective-permute-start | bytes 7688 | tf_op jit(solution)/shard_map/ppermute | solution.py:22
  63.3 18.9 %collective-permute-start.10 = (f32[64,1,128]{2,1,0:T(1,128)S(1)}, f32[64,1,128]{2,1,0:T(1,128)S(1)}, u32[]{:S(2)}, u32[]{:S(2)}) collective-permute-start(f32[64,1,128]{2,1,0:T(1,128)S(1)} %get-tuple-element.114), channel_id=1, source_target_pairs={{8,0},{16,8},{24,16},{9,1},{17,9},{25,17},{10,2},{18,10},{26,18},{... | collective-permute-start | bytes 98312 | tf_op jit(solution)/shard_map/ppermute | solution.py:22
  64.6 17.6 %collective-permute-start.11 = (f32[64,1,128]{2,1,0:T(1,128)S(1)}, f32[64,1,128]{2,1,0:T(1,128)S(1)}, u32[]{:S(2)}, u32[]{:S(2)}) collective-permute-start(f32[64,1,128]{2,1,0:T(1,128)S(1)} %get-tuple-element.115), channel_id=1, source_target_pairs={{0,8},{8,16},{16,24},{1,9},{9,17},{17,25},{2,10},{10,18},{18,26},{... | collective-permute-start | bytes 98312 | tf_op jit(solution)/shard_map/ppermute | solution.py:21
  69.3 12.9 %collective-permute-start.8 = (f32[64,8,1]{2,1,0:T(8,128)S(1)}, f32[64,8,1]{2,1,0:T(8,128)S(1)}, u32[]{:S(2)}, u32[]{:S(2)}) collective-permute-start(f32[64,8,1]{2,1,0:T(8,128)S(1)} %get-tuple-element.112), channel_id=1, source_target_pairs={{2,0},{4,2},{6,4},{0,6},{3,1},{5,3},{7,5},{1,7},{10,8},{12,10},{14... | collective-permute-start | bytes 6152 | tf_op jit(solution)/shard_map/ppermute | solution.py:22
  71.4 10.8 %collective-permute-start.9 = (f32[64,8,1]{2,1,0:T(8,128)S(1)}, f32[64,8,1]{2,1,0:T(8,128)S(1)}, u32[]{:S(2)}, u32[]{:S(2)}) collective-permute-start(f32[64,8,1]{2,1,0:T(8,128)S(1)} %get-tuple-element.113), channel_id=1, source_target_pairs={{0,2},{2,4},{4,6},{6,0},{1,3},{3,5},{5,7},{7,1},{8,10},{10,12},{12... | collective-permute-start | bytes 6152 | tf_op jit(solution)/shard_map/ppermute | solution.py:21
  89.7 16.4 %collective-permute-start.14 = (f32[64,10,1]{2,1,0:T(8,128)S(1)}, f32[64,10,1]{2,1,0:T(8,128)S(1)}, u32[]{:S(2)}, u32[]{:S(2)}) collective-permute-start(f32[64,10,1]{2,1,0:T(8,128)S(1)} %get-tuple-element.54), channel_id=1, source_target_pairs={{0,2},{2,4},{4,6},{6,0},{1,3},{3,5},{5,7},{7,1},{8,10},{10,12},{12... | collective-permute-start | bytes 7688 | tf_op jit(solution)/shard_map/ppermute | solution.py:21
  90.0 21.6 %collective-permute-start.15 = (f32[64,10,1]{2,1,0:T(8,128)S(1)}, f32[64,10,1]{2,1,0:T(8,128)S(1)}, u32[]{:S(2)}, u32[]{:S(2)}) collective-permute-start(f32[64,10,1]{2,1,0:T(8,128)S(1)} %get-tuple-element.55), channel_id=1, source_target_pairs={{2,0},{4,2},{6,4},{0,6},{3,1},{5,3},{7,5},{1,7},{10,8},{12,10},{14... | collective-permute-start | bytes 7688 | tf_op jit(solution)/shard_map/ppermute | solution.py:22
  112.7 19.3 %collective-permute-start.18 = (f32[64,1,128]{2,1,0:T(1,128)S(1)}, f32[64,1,128]{2,1,0:T(1,128)S(1)}, u32[]{:S(2)}, u32[]{:S(2)}) collective-permute-start(f32[64,1,128]{2,1,0:T(1,128)S(1)} %get-tuple-element.108), channel_id=1, source_target_pairs={{8,0},{16,8},{24,16},{9,1},{17,9},{25,17},{10,2},{18,10},{26,18},{... | collective-permute-start | bytes 98312 | tf_op jit(solution)/shard_map/ppermute | solution.py:22
  114.0 18.0 %collective-permute-start.19 = (f32[64,1,128]{2,1,0:T(1,128)S(1)}, f32[64,1,128]{2,1,0:T(1,128)S(1)}, u32[]{:S(2)}, u32[]{:S(2)}) collective-permute-start(f32[64,1,128]{2,1,0:T(1,128)S(1)} %get-tuple-element.109), channel_id=1, source_target_pairs={{0,8},{8,16},{16,24},{1,9},{9,17},{17,25},{2,10},{10,18},{18,26},{... | collective-permute-start | bytes 98312 | tf_op jit(solution)/shard_map/ppermute | solution.py:21
  118.7 13.3 %collective-permute-start.16 = (f32[64,8,1]{2,1,0:T(8,128)S(1)}, f32[64,8,1]{2,1,0:T(8,128)S(1)}, u32[]{:S(2)}, u32[]{:S(2)}) collective-permute-start(f32[64,8,1]{2,1,0:T(8,128)S(1)} %get-tuple-element.106), channel_id=1, source_target_pairs={{2,0},{4,2},{6,4},{0,6},{3,1},{5,3},{7,5},{1,7},{10,8},{12,10},{14... | collective-permute-start | bytes 6152 | tf_op jit(solution)/shard_map/ppermute | solution.py:22
  121.7 10.4 %collective-permute-start.17 = (f32[64,8,1]{2,1,0:T(8,128)S(1)}, f32[64,8,1]{2,1,0:T(8,128)S(1)}, u32[]{:S(2)}, u32[]{:S(2)}) collective-permute-start(f32[64,8,1]{2,1,0:T(8,128)S(1)} %get-tuple-element.107), channel_id=1, source_target_pairs={{0,2},{2,4},{4,6},{6,0},{1,3},{3,5},{5,7},{7,1},{8,10},{10,12},{12... | collective-permute-start | bytes 6152 | tf_op jit(solution)/shard_map/ppermute | solution.py:21
  139.8 16.6 %collective-permute-start.22 = (f32[64,10,1]{2,1,0:T(8,128)}, f32[64,10,1]{2,1,0:T(8,128)S(1)}, u32[]{:S(2)}, u32[]{:S(2)}) collective-permute-start(f32[64,10,1]{2,1,0:T(8,128)} %get-tuple-element.52), channel_id=1, source_target_pairs={{0,2},{2,4},{4,6},{6,0},{1,3},{3,5},{5,7},{7,1},{8,10},{10,12},{12... | collective-permute-start | bytes 7688 | tf_op jit(solution)/shard_map/ppermute | solution.py:21
  140.3 21.7 %collective-permute-start.23 = (f32[64,10,1]{2,1,0:T(8,128)}, f32[64,10,1]{2,1,0:T(8,128)}, u32[]{:S(2)}, u32[]{:S(2)}) collective-permute-start(f32[64,10,1]{2,1,0:T(8,128)} %get-tuple-element.53), channel_id=1, source_target_pairs={{2,0},{4,2},{6,4},{0,6},{3,1},{5,3},{7,5},{1,7},{10,8},{12,10},{14... | collective-permute-start | bytes 7688 | tf_op jit(solution)/shard_map/ppermute | solution.py:22
  144.3 89.0 %all-to-all-start.1 = ((f32[2,16,8]{2,0,1:T(2,128)}), f32[2,16,8]{2,0,1:T(2,128)}, u32[]{:S(2)}, u32[]{:S(2)}) async-start(f32[2,16,8]{2,0,1:T(2,128)} %bitcast.16), calls=%async_computation.1 | async-start | bytes 32768 | tf_op jit(solution)/shard_map/all_to_all | solution.py:95
  164.3 13.8 %collective-permute-start.24 = (f32[64,8,1]{2,1,0:T(8,128)S(1)}, f32[64,8,1]{2,1,0:T(8,128)S(1)}, u32[]{:S(2)}, u32[]{:S(2)}) collective-permute-start(f32[64,8,1]{2,1,0:T(8,128)S(1)} %get-tuple-element.100), channel_id=1, source_target_pairs={{2,0},{4,2},{6,4},{0,6},{3,1},{5,3},{7,5},{1,7},{10,8},{12,10},{14... | collective-permute-start | bytes 6152 | tf_op jit(solution)/shard_map/ppermute | solution.py:22
  167.2 10.9 %collective-permute-start.25 = (f32[64,8,1]{2,1,0:T(8,128)S(1)}, f32[64,8,1]{2,1,0:T(8,128)S(1)}, u32[]{:S(2)}, u32[]{:S(2)}) collective-permute-start(f32[64,8,1]{2,1,0:T(8,128)S(1)} %get-tuple-element.101), channel_id=1, source_target_pairs={{0,2},{2,4},{4,6},{6,0},{1,3},{3,5},{5,7},{7,1},{8,10},{10,12},{12... | collective-permute-start | bytes 6152 | tf_op jit(solution)/shard_map/ppermute | solution.py:21
  167.2 10.9 %collective-permute-start.26 = (f32[64,1,128]{2,1,0:T(1,128)S(1)}, f32[64,1,128]{2,1,0:T(1,128)S(1)}, u32[]{:S(2)}, u32[]{:S(2)}) collective-permute-start(f32[64,1,128]{2,1,0:T(1,128)S(1)} %get-tuple-element.102), channel_id=1, source_target_pairs={{8,0},{16,8},{24,16},{9,1},{17,9},{25,17},{10,2},{18,10},{26,18},{... | collective-permute-start | bytes 98312 | tf_op jit(solution)/shard_map/ppermute | solution.py:22
  184.2 16.6 %collective-permute-start.30 = (f32[64,10,1]{2,1,0:T(8,128)S(1)}, f32[64,10,1]{2,1,0:T(8,128)S(1)}, u32[]{:S(2)}, u32[]{:S(2)}) collective-permute-start(f32[64,10,1]{2,1,0:T(8,128)S(1)} %get-tuple-element.50), channel_id=1, source_target_pairs={{0,2},{2,4},{4,6},{6,0},{1,3},{3,5},{5,7},{7,1},{8,10},{10,12},{12... | collective-permute-start | bytes 7688 | tf_op jit(solution)/shard_map/ppermute | solution.py:21
  184.9 22.1 %collective-permute-start.31 = (f32[64,10,1]{2,1,0:T(8,128)S(1)}, f32[64,10,1]{2,1,0:T(8,128)S(1)}, u32[]{:S(2)}, u32[]{:S(2)}) collective-permute-start(f32[64,10,1]{2,1,0:T(8,128)S(1)} %get-tuple-element.51), channel_id=1, source_target_pairs={{2,0},{4,2},{6,4},{0,6},{3,1},{5,3},{7,5},{1,7},{10,8},{12,10},{14... | collective-permute-start | bytes 7688 | tf_op jit(solution)/shard_map/ppermute | solution.py:22
  208.2 13.9 %collective-permute-start.32 = (f32[64,8,1]{2,1,0:T(8,128)S(1)}, f32[64,8,1]{2,1,0:T(8,128)S(1)}, u32[]{:S(2)}, u32[]{:S(2)}) collective-permute-start(f32[64,8,1]{2,1,0:T(8,128)S(1)} %get-tuple-element.94), channel_id=1, source_target_pairs={{2,0},{4,2},{6,4},{0,6},{3,1},{5,3},{7,5},{1,7},{10,8},{12,10},{14... | collective-permute-start | bytes 6152 | tf_op jit(solution)/shard_map/ppermute | solution.py:22
  210.3 11.8 %collective-permute-start.33 = (f32[64,8,1]{2,1,0:T(8,128)S(1)}, f32[64,8,1]{2,1,0:T(8,128)S(1)}, u32[]{:S(2)}, u32[]{:S(2)}) collective-permute-start(f32[64,8,1]{2,1,0:T(8,128)S(1)} %get-tuple-element.95), channel_id=1, source_target_pairs={{0,2},{2,4},{4,6},{6,0},{1,3},{3,5},{5,7},{7,1},{8,10},{10,12},{12... | collective-permute-start | bytes 6152 | tf_op jit(solution)/shard_map/ppermute | solution.py:21
  210.4 11.7 %collective-permute-start.34 = (f32[64,1,128]{2,1,0:T(1,128)S(1)}, f32[64,1,128]{2,1,0:T(1,128)S(1)}, u32[]{:S(2)}, u32[]{:S(2)}) collective-permute-start(f32[64,1,128]{2,1,0:T(1,128)S(1)} %get-tuple-element.96), channel_id=1, source_target_pairs={{8,0},{16,8},{24,16},{9,1},{17,9},{25,17},{10,2},{18,10},{26,18},{... | collective-permute-start | bytes 98312 | tf_op jit(solution)/shard_map/ppermute | solution.py:22
  211.7 10.4 %collective-permute-start.35 = (f32[64,1,128]{2,1,0:T(1,128)S(1)}, f32[64,1,128]{2,1,0:T(1,128)S(1)}, u32[]{:S(2)}, u32[]{:S(2)}) collective-permute-start(f32[64,1,128]{2,1,0:T(1,128)S(1)} %get-tuple-element.97), channel_id=1, source_target_pairs={{0,8},{8,16},{16,24},{1,9},{9,17},{17,25},{2,10},{10,18},{18,26},{... | collective-permute-start | bytes 98312 | tf_op jit(solution)/shard_map/ppermute | solution.py:21
  229.4 16.8 %collective-permute-start.38 = (f32[64,10,1]{2,1,0:T(8,128)}, f32[64,10,1]{2,1,0:T(8,128)S(1)}, u32[]{:S(2)}, u32[]{:S(2)}) collective-permute-start(f32[64,10,1]{2,1,0:T(8,128)} %get-tuple-element.48), channel_id=1, source_target_pairs={{0,2},{2,4},{4,6},{6,0},{1,3},{3,5},{5,7},{7,1},{8,10},{10,12},{12... | collective-permute-start | bytes 7688 | tf_op jit(solution)/shard_map/ppermute | solution.py:21
  230.0 22.8 %collective-permute-start.39 = (f32[64,10,1]{2,1,0:T(8,128)S(1)}, f32[64,10,1]{2,1,0:T(8,128)}, u32[]{:S(2)}, u32[]{:S(2)}) collective-permute-start(f32[64,10,1]{2,1,0:T(8,128)S(1)} %get-tuple-element.49), channel_id=1, source_target_pairs={{2,0},{4,2},{6,4},{0,6},{3,1},{5,3},{7,5},{1,7},{10,8},{12,10},{14... | collective-permute-start | bytes 7688 | tf_op jit(solution)/shard_map/ppermute | solution.py:22
  233.2 31.0 %all-to-all-start = ((f32[2,16,8]{2,0,1:T(2,128)}), f32[2,16,8]{2,0,1:T(2,128)}, u32[]{:S(2)}, u32[]{:S(2)}) async-start(f32[2,16,8]{2,0,1:T(2,128)} %bitcast.208), calls=%async_computation | async-start | bytes 32768 | tf_op jit(solution)/shard_map/all_to_all | solution.py:96
  237.4 145.1 %all-reduce.7.cloned.1.call-start = ((), (), s32[]{:S(2)}) async-start(), calls=%async_computation.5 | async-start | bytes 262144 | tf_op jit(solution)/shard_map/psum | solution.py:112
  255.1 13.8 %collective-permute-start.40 = (f32[64,8,1]{2,1,0:T(8,128)S(1)}, f32[64,8,1]{2,1,0:T(8,128)S(1)}, u32[]{:S(2)}, u32[]{:S(2)}) collective-permute-start(f32[64,8,1]{2,1,0:T(8,128)S(1)} %get-tuple-element.88), channel_id=1, source_target_pairs={{2,0},{4,2},{6,4},{0,6},{3,1},{5,3},{7,5},{1,7},{10,8},{12,10},{14... | collective-permute-start | bytes 6152 | tf_op jit(solution)/shard_map/ppermute | solution.py:22
  257.2 11.7 %collective-permute-start.41 = (f32[64,8,1]{2,1,0:T(8,128)S(1)}, f32[64,8,1]{2,1,0:T(8,128)S(1)}, u32[]{:S(2)}, u32[]{:S(2)}) collective-permute-start(f32[64,8,1]{2,1,0:T(8,128)S(1)} %get-tuple-element.89), channel_id=1, source_target_pairs={{0,2},{2,4},{4,6},{6,0},{1,3},{3,5},{5,7},{7,1},{8,10},{10,12},{12... | collective-permute-start | bytes 6152 | tf_op jit(solution)/shard_map/ppermute | solution.py:21
  257.8 11.1 %collective-permute-start.42 = (f32[64,1,128]{2,1,0:T(1,128)}, f32[64,1,128]{2,1,0:T(1,128)}, u32[]{:S(2)}, u32[]{:S(2)}) collective-permute-start(f32[64,1,128]{2,1,0:T(1,128)} %get-tuple-element.90), channel_id=1, source_target_pairs={{8,0},{16,8},{24,16},{9,1},{17,9},{25,17},{10,2},{18,10},{26,18},{... | collective-permute-start | bytes 98312 | tf_op jit(solution)/shard_map/ppermute | solution.py:22
  277.2 130.5 %all-gather.3.cloned.1.call-start = ((), (), s32[]{:S(2)}) async-start(), calls=%async_computation.2 | async-start | bytes 1572864 | tf_op jit(solution)/shard_map/all_gather | solution.py:120
  277.8 485.1 %all-reduce.5.cloned.1.call-start = ((), (), s32[]{:S(2)}) async-start(), calls=%async_computation.4 | async-start | bytes 262144 | tf_op jit(solution)/shard_map/psum | solution.py:112
  417.1 16.6 %collective-permute-start.46 = (f32[64,10,1]{2,1,0:T(8,128)S(1)}, f32[64,10,1]{2,1,0:T(8,128)S(1)}, u32[]{:S(2)}, u32[]{:S(2)}) collective-permute-start(f32[64,10,1]{2,1,0:T(8,128)S(1)} %get-tuple-element.44), channel_id=1, source_target_pairs={{0,2},{2,4},{4,6},{6,0},{1,3},{3,5},{5,7},{7,1},{8,10},{10,12},{12... | collective-permute-start | bytes 7688 | tf_op jit(solution)/shard_map/ppermute | solution.py:21
  417.9 21.4 %collective-permute-start.47 = (f32[64,10,1]{2,1,0:T(8,128)S(1)}, f32[64,10,1]{2,1,0:T(8,128)S(1)}, u32[]{:S(2)}, u32[]{:S(2)}) collective-permute-start(f32[64,10,1]{2,1,0:T(8,128)S(1)} %get-tuple-element.45), channel_id=1, source_target_pairs={{2,0},{4,2},{6,4},{0,6},{3,1},{5,3},{7,5},{1,7},{10,8},{12,10},{14... | collective-permute-start | bytes 7688 | tf_op jit(solution)/shard_map/ppermute | solution.py:22
  440.4 18.8 %collective-permute-start.50 = (f32[64,1,128]{2,1,0:T(1,128)S(1)}, f32[64,1,128]{2,1,0:T(1,128)S(1)}, u32[]{:S(2)}, u32[]{:S(2)}) collective-permute-start(f32[64,1,128]{2,1,0:T(1,128)S(1)} %get-tuple-element.84), channel_id=1, source_target_pairs={{8,0},{16,8},{24,16},{9,1},{17,9},{25,17},{10,2},{18,10},{26,18},{... | collective-permute-start | bytes 98312 | tf_op jit(solution)/shard_map/ppermute | solution.py:22
  441.7 17.6 %collective-permute-start.51 = (f32[64,1,128]{2,1,0:T(1,128)S(1)}, f32[64,1,128]{2,1,0:T(1,128)S(1)}, u32[]{:S(2)}, u32[]{:S(2)}) collective-permute-start(f32[64,1,128]{2,1,0:T(1,128)S(1)} %get-tuple-element.85), channel_id=1, source_target_pairs={{0,8},{8,16},{16,24},{1,9},{9,17},{17,25},{2,10},{10,18},{18,26},{... | collective-permute-start | bytes 98312 | tf_op jit(solution)/shard_map/ppermute | solution.py:21
  446.6 12.6 %collective-permute-start.48 = (f32[64,8,1]{2,1,0:T(8,128)S(1)}, f32[64,8,1]{2,1,0:T(8,128)S(1)}, u32[]{:S(2)}, u32[]{:S(2)}) collective-permute-start(f32[64,8,1]{2,1,0:T(8,128)S(1)} %get-tuple-element.82), channel_id=1, source_target_pairs={{2,0},{4,2},{6,4},{0,6},{3,1},{5,3},{7,5},{1,7},{10,8},{12,10},{14... | collective-permute-start | bytes 6152 | tf_op jit(solution)/shard_map/ppermute | solution.py:22
  448.8 10.4 %collective-permute-start.49 = (f32[64,8,1]{2,1,0:T(8,128)S(1)}, f32[64,8,1]{2,1,0:T(8,128)S(1)}, u32[]{:S(2)}, u32[]{:S(2)}) collective-permute-start(f32[64,8,1]{2,1,0:T(8,128)S(1)} %get-tuple-element.83), channel_id=1, source_target_pairs={{0,2},{2,4},{4,6},{6,0},{1,3},{3,5},{5,7},{7,1},{8,10},{10,12},{12... | collective-permute-start | bytes 6152 | tf_op jit(solution)/shard_map/ppermute | solution.py:21
  466.7 16.6 %collective-permute-start.54 = (f32[64,10,1]{2,1,0:T(8,128)S(1)}, f32[64,10,1]{2,1,0:T(8,128)S(1)}, u32[]{:S(2)}, u32[]{:S(2)}) collective-permute-start(f32[64,10,1]{2,1,0:T(8,128)S(1)} %get-tuple-element.42), channel_id=1, source_target_pairs={{0,2},{2,4},{4,6},{6,0},{1,3},{3,5},{5,7},{7,1},{8,10},{10,12},{12... | collective-permute-start | bytes 7688 | tf_op jit(solution)/shard_map/ppermute | solution.py:21
  468.1 21.7 %collective-permute-start.55 = (f32[64,10,1]{2,1,0:T(8,128)S(1)}, f32[64,10,1]{2,1,0:T(8,128)S(1)}, u32[]{:S(2)}, u32[]{:S(2)}) collective-permute-start(f32[64,10,1]{2,1,0:T(8,128)S(1)} %get-tuple-element.43), channel_id=1, source_target_pairs={{2,0},{4,2},{6,4},{0,6},{3,1},{5,3},{7,5},{1,7},{10,8},{12,10},{14... | collective-permute-start | bytes 7688 | tf_op jit(solution)/shard_map/ppermute | solution.py:22
  490.8 19.2 %collective-permute-start.58 = (f32[64,1,128]{2,1,0:T(1,128)S(1)}, f32[64,1,128]{2,1,0:T(1,128)S(1)}, u32[]{:S(2)}, u32[]{:S(2)}) collective-permute-start(f32[64,1,128]{2,1,0:T(1,128)S(1)} %get-tuple-element.78), channel_id=1, source_target_pairs={{8,0},{16,8},{24,16},{9,1},{17,9},{25,17},{10,2},{18,10},{26,18},{... | collective-permute-start | bytes 98312 | tf_op jit(solution)/shard_map/ppermute | solution.py:22
  492.1 17.9 %collective-permute-start.59 = (f32[64,1,128]{2,1,0:T(1,128)S(1)}, f32[64,1,128]{2,1,0:T(1,128)S(1)}, u32[]{:S(2)}, u32[]{:S(2)}) collective-permute-start(f32[64,1,128]{2,1,0:T(1,128)S(1)} %get-tuple-element.79), channel_id=1, source_target_pairs={{0,8},{8,16},{16,24},{1,9},{9,17},{17,25},{2,10},{10,18},{18,26},{... | collective-permute-start | bytes 98312 | tf_op jit(solution)/shard_map/ppermute | solution.py:21
  499.4 10.6 %collective-permute-start.57 = (f32[64,8,1]{2,1,0:T(8,128)S(1)}, f32[64,8,1]{2,1,0:T(8,128)S(1)}, u32[]{:S(2)}, u32[]{:S(2)}) collective-permute-start(f32[64,8,1]{2,1,0:T(8,128)S(1)} %get-tuple-element.77), channel_id=1, source_target_pairs={{0,2},{2,4},{4,6},{6,0},{1,3},{3,5},{5,7},{7,1},{8,10},{10,12},{12... | collective-permute-start | bytes 6152 | tf_op jit(solution)/shard_map/ppermute | solution.py:21
  516.6 16.6 %collective-permute-start.62 = (f32[64,10,1]{2,1,0:T(8,128)S(1)}, f32[64,10,1]{2,1,0:T(8,128)S(1)}, u32[]{:S(2)}, u32[]{:S(2)}) collective-permute-start(f32[64,10,1]{2,1,0:T(8,128)S(1)} %get-tuple-element.40), channel_id=1, source_target_pairs={{0,2},{2,4},{4,6},{6,0},{1,3},{3,5},{5,7},{7,1},{8,10},{10,12},{12... | collective-permute-start | bytes 7688 | tf_op jit(solution)/shard_map/ppermute | solution.py:21
  518.1 21.4 %collective-permute-start.63 = (f32[64,10,1]{2,1,0:T(8,128)S(1)}, f32[64,10,1]{2,1,0:T(8,128)S(1)}, u32[]{:S(2)}, u32[]{:S(2)}) collective-permute-start(f32[64,10,1]{2,1,0:T(8,128)S(1)} %get-tuple-element.41), channel_id=1, source_target_pairs={{2,0},{4,2},{6,4},{0,6},{3,1},{5,3},{7,5},{1,7},{10,8},{12,10},{14... | collective-permute-start | bytes 7688 | tf_op jit(solution)/shard_map/ppermute | solution.py:22
  540.6 19.4 %collective-permute-start.66 = (f32[64,1,128]{2,1,0:T(1,128)S(1)}, f32[64,1,128]{2,1,0:T(1,128)S(1)}, u32[]{:S(2)}, u32[]{:S(2)}) collective-permute-start(f32[64,1,128]{2,1,0:T(1,128)S(1)} %get-tuple-element.72), channel_id=1, source_target_pairs={{8,0},{16,8},{24,16},{9,1},{17,9},{25,17},{10,2},{18,10},{26,18},{... | collective-permute-start | bytes 98312 | tf_op jit(solution)/shard_map/ppermute | solution.py:22
  541.9 18.1 %collective-permute-start.67 = (f32[64,1,128]{2,1,0:T(1,128)S(1)}, f32[64,1,128]{2,1,0:T(1,128)S(1)}, u32[]{:S(2)}, u32[]{:S(2)}) collective-permute-start(f32[64,1,128]{2,1,0:T(1,128)S(1)} %get-tuple-element.73), channel_id=1, source_target_pairs={{0,8},{8,16},{16,24},{1,9},{9,17},{17,25},{2,10},{10,18},{18,26},{... | collective-permute-start | bytes 98312 | tf_op jit(solution)/shard_map/ppermute | solution.py:21
  549.4 10.6 %collective-permute-start.65 = (f32[64,8,1]{2,1,0:T(8,128)S(1)}, f32[64,8,1]{2,1,0:T(8,128)S(1)}, u32[]{:S(2)}, u32[]{:S(2)}) collective-permute-start(f32[64,8,1]{2,1,0:T(8,128)S(1)} %get-tuple-element.71), channel_id=1, source_target_pairs={{0,2},{2,4},{4,6},{6,0},{1,3},{3,5},{5,7},{7,1},{8,10},{10,12},{12... | collective-permute-start | bytes 6152 | tf_op jit(solution)/shard_map/ppermute | solution.py:21
  566.7 16.6 %collective-permute-start.70 = (f32[64,10,1]{2,1,0:T(8,128)S(1)}, f32[64,10,1]{2,1,0:T(8,128)S(1)}, u32[]{:S(2)}, u32[]{:S(2)}) collective-permute-start(f32[64,10,1]{2,1,0:T(8,128)S(1)} %get-tuple-element.38), channel_id=1, source_target_pairs={{0,2},{2,4},{4,6},{6,0},{1,3},{3,5},{5,7},{7,1},{8,10},{10,12},{12... | collective-permute-start | bytes 7688 | tf_op jit(solution)/shard_map/ppermute | solution.py:21
  568.2 19.6 %collective-permute-start.71 = (f32[64,10,1]{2,1,0:T(8,128)S(1)}, f32[64,10,1]{2,1,0:T(8,128)S(1)}, u32[]{:S(2)}, u32[]{:S(2)}) collective-permute-start(f32[64,10,1]{2,1,0:T(8,128)S(1)} %get-tuple-element.39), channel_id=1, source_target_pairs={{2,0},{4,2},{6,4},{0,6},{3,1},{5,3},{7,5},{1,7},{10,8},{12,10},{14... | collective-permute-start | bytes 7688 | tf_op jit(solution)/shard_map/ppermute | solution.py:22
  589.0 19.3 %collective-permute-start.74 = (f32[64,1,128]{2,1,0:T(1,128)S(1)}, f32[64,1,128]{2,1,0:T(1,128)S(1)}, u32[]{:S(2)}, u32[]{:S(2)}) collective-permute-start(f32[64,1,128]{2,1,0:T(1,128)S(1)} %get-tuple-element.66), channel_id=1, source_target_pairs={{8,0},{16,8},{24,16},{9,1},{17,9},{25,17},{10,2},{18,10},{26,18},{... | collective-permute-start | bytes 98312 | tf_op jit(solution)/shard_map/ppermute | solution.py:22
  590.3 18.0 %collective-permute-start.75 = (f32[64,1,128]{2,1,0:T(1,128)S(1)}, f32[64,1,128]{2,1,0:T(1,128)S(1)}, u32[]{:S(2)}, u32[]{:S(2)}) collective-permute-start(f32[64,1,128]{2,1,0:T(1,128)S(1)} %get-tuple-element.67), channel_id=1, source_target_pairs={{0,8},{8,16},{16,24},{1,9},{9,17},{17,25},{2,10},{10,18},{18,26},{... | collective-permute-start | bytes 98312 | tf_op jit(solution)/shard_map/ppermute | solution.py:21
  595.0 10.2 %collective-permute-start.72 = (f32[64,8,1]{2,1,0:T(8,128)S(1)}, f32[64,8,1]{2,1,0:T(8,128)S(1)}, u32[]{:S(2)}, u32[]{:S(2)}) collective-permute-start(f32[64,8,1]{2,1,0:T(8,128)S(1)} %get-tuple-element.64), channel_id=1, source_target_pairs={{2,0},{4,2},{6,4},{0,6},{3,1},{5,3},{7,5},{1,7},{10,8},{12,10},{14... | collective-permute-start | bytes 6152 | tf_op jit(solution)/shard_map/ppermute | solution.py:22
  597.8 10.5 %collective-permute-start.73 = (f32[64,8,1]{2,1,0:T(8,128)S(1)}, f32[64,8,1]{2,1,0:T(8,128)S(1)}, u32[]{:S(2)}, u32[]{:S(2)}) collective-permute-start(f32[64,8,1]{2,1,0:T(8,128)S(1)} %get-tuple-element.65), channel_id=1, source_target_pairs={{0,2},{2,4},{4,6},{6,0},{1,3},{3,5},{5,7},{7,1},{8,10},{10,12},{12... | collective-permute-start | bytes 6152 | tf_op jit(solution)/shard_map/ppermute | solution.py:21
  615.0 16.0 %collective-permute-start.78 = (f32[64,10,1]{2,1,0:T(8,128)S(1)}, f32[64,10,1]{2,1,0:T(8,128)S(1)}, u32[]{:S(2)}, u32[]{:S(2)}) collective-permute-start(f32[64,10,1]{2,1,0:T(8,128)S(1)} %get-tuple-element.36), channel_id=1, source_target_pairs={{0,2},{2,4},{4,6},{6,0},{1,3},{3,5},{5,7},{7,1},{8,10},{10,12},{12... | collective-permute-start | bytes 7688 | tf_op jit(solution)/shard_map/ppermute | solution.py:21
  616.6 18.8 %collective-permute-start.79 = (f32[64,10,1]{2,1,0:T(8,128)S(1)}, f32[64,10,1]{2,1,0:T(8,128)S(1)}, u32[]{:S(2)}, u32[]{:S(2)}) collective-permute-start(f32[64,10,1]{2,1,0:T(8,128)S(1)} %get-tuple-element.37), channel_id=1, source_target_pairs={{2,0},{4,2},{6,4},{0,6},{3,1},{5,3},{7,5},{1,7},{10,8},{12,10},{14... | collective-permute-start | bytes 7688 | tf_op jit(solution)/shard_map/ppermute | solution.py:22
  638.7 10.9 %collective-permute-start.81 = (f32[64,8,1]{2,1,0:T(8,128)S(1)}, f32[64,8,1]{2,1,0:T(8,128)S(1)}, u32[]{:S(2)}, u32[]{:S(2)}) collective-permute-start(f32[64,8,1]{2,1,0:T(8,128)S(1)} %get-tuple-element.59), channel_id=1, source_target_pairs={{0,2},{2,4},{4,6},{6,0},{1,3},{3,5},{5,7},{7,1},{8,10},{10,12},{12... | collective-permute-start | bytes 6152 | tf_op jit(solution)/shard_map/ppermute | solution.py:21
  638.8 10.9 %collective-permute-start.82 = (f32[64,1,128]{2,1,0:T(1,128)S(1)}, f32[64,1,128]{2,1,0:T(1,128)S(1)}, u32[]{:S(2)}, u32[]{:S(2)}) collective-permute-start(f32[64,1,128]{2,1,0:T(1,128)S(1)} %get-tuple-element.60), channel_id=1, source_target_pairs={{8,0},{16,8},{24,16},{9,1},{17,9},{25,17},{10,2},{18,10},{26,18},{... | collective-permute-start | bytes 98312 | tf_op jit(solution)/shard_map/ppermute | solution.py:22
  657.0 131.1 %all-gather.5.cloned.1.call-start = ((), (), s32[]{:S(2)}) async-start(), calls=%async_computation.3 | async-start | bytes 1572864 | tf_op jit(solution)/shard_map/all_gather | solution.py:120
  (53 other events, 585.2 us)
Sparse Core Ops, SparseCore 0:
  277.3 105.1 all-reduce.6
  657.2 105.7 all-reduce.4
Sparse Core Ops, SparseCore 1:
  279.2 8.2 all-gather.2
  659.1 8.8 all-gather.4
where the time goes:
time: 810 us; the launch traced here: 800 us
  waiting for transfers between devices  505 us (62%)
  starting transfers between devices  173 us (21%)
  other arithmetic  69.1 us (9%)
  local copies, waits for them, and re-layouts  25.9 us (3%)
  between operations  16.5 us (2%)
    psum x2, waiting for transfers between devices, per_device(): gram_part, cross_part = lax.psum((gram_part, cross_part), ('lat', 'lon'))  210 us
    ppermute x42, waiting for transfers between devices, padded_2(): before = lax.ppermute(last, axis, up)  150 us
    ppermute x42, waiting for transfers between devices, padded_2(): after = lax.ppermute(leading, axis, down)  145 us
    ppermute x42, starting transfers between devices, padded_2(): before = lax.ppermute(last, axis, up)  83.4 us
    ppermute x42, starting transfers between devices, padded_2(): after = lax.ppermute(leading, axis, down)  80.4 us
    another operation x6, other arithmetic, solve_weights(): factor = jnp.linalg.cholesky(system)  24.8 us
    another operation x4, other arithmetic, solve_weights(): jax.scipy.linalg.cho_solve((factor, True), cross_part) / math.sqrt(members)  21 us
  transfers between devices with their start and end apart: 90, of which 57 were waited for; matrix products, arithmetic and copies ran while one was open for 8% of the time, Pallas kernels for 0%

commit v1 on v0

--- a/solution.py
+++ b/solution.py
@@ -3,12 +3,17 @@
 import jax.numpy as jnp
 from jax import lax
 from jax.sharding import PartitionSpec as P
+from jax.lax import psum
 
 STEPS = 6
 ITERS = 2
 depth_step = 0.7
 gravity_step = 0.7
 coriolis = 0.1
+
+
+def close_side_now(sheet, net_axis, along_axis):
+    return psum(psum(sheet, net_axis), along_axis)
 
 
 def padded_2(value, sides, width, wrap):
@@ -109,7 +114,7 @@
         gram_part, cross_part = gram_terms(
             gathered.reshape(-1, members), observed.reshape(-1), precision.reshape(-1)
         )
-        gram_part, cross_part = lax.psum((gram_part, cross_part), ("lat", "lon"))
+        gram_part, cross_part = close_side_now((gram_part, cross_part), "lon", "lat")
         centred = solve_weights(gram_part, cross_part)
         local_weights = lax.dynamic_slice_in_dim(
             centred, member_block * members_here, members_here, 1

time: 810 us -> 760 us (0.938)
  waiting for transfers between devices: 505 us -> 455 us
    psum x2 -> x4, waiting for transfers between devices: 210 us -> 156 us  [close_side_now(): return psum(psum(sheet, net_axis), along_axis)]
  transfers between devices with their start and end apart: 90 -> 92, of which waited for: 57 -> 58; matrix products, arithmetic and copies ran while one was open for 8% -> 9% of each run, Pallas kernels for 0% -> 0%
where the time goes in v1:
time: 760 us; the launch traced here: 750 us
  waiting for transfers between devices  455 us (60%)
  starting transfers between devices  172 us (23%)
  other arithmetic  69.2 us (9%)
  local copies, waits for them, and re-layouts  25.9 us (3%)
  between operations  16.2 us (2%)
    psum x4, waiting for transfers between devices, close_side_now(): return psum(psum(sheet, net_axis), along_axis)  156 us
    ppermute x42, waiting for transfers between devices, padded_2(): after = lax.ppermute(leading, axis, down)  150 us
    ppermute x42, waiting for transfers between devices, padded_2(): before = lax.ppermute(last, axis, up)  148 us
    ppermute x42, starting transfers between devices, padded_2(): before = lax.ppermute(last, axis, up)  85.1 us
    ppermute x42, starting transfers between devices, padded_2(): after = lax.ppermute(leading, axis, down)  78.4 us
    another operation x6, other arithmetic, solve_weights(): factor = jnp.linalg.cholesky(system)  24.8 us
    another operation x4, other arithmetic, solve_weights(): jax.scipy.linalg.cho_solve((factor, True), cross_part) / math.sqrt(members)  21 us
  transfers between devices with their start and end apart: 92, of which 58 were waited for; matrix products, arithmetic and copies ran while one was open for 9% of the time, Pallas kernels for 0%

profile of v1, /device:TPU:0, one launch (start us, length us, event | category | flops | bytes accessed | tf_op | source)
XLA Modules:
  0.0 749.6 jit_solution(6522170547363656495)
XLA Ops:
  9.5 5.5 collective-permute-start.3
  15.3 4.2 collective-permute-start
  19.6 6.5 collective-permute-done
  26.2 4.8 collective-permute-done.1
  42.6 12.8 %collective-permute-done.6 = f32[64,10,1]{2,1,0:T(8,128)S(1)} collective-permute-done((f32[64,10,1]{2,1,0:T(8,128)S(1)}, f32[64,10,1]{2,1,0:T(8,128)S(1)}, u32[]{:S(2)}, u32[]{:S(2)}) %collective-permute-start.6) | collective-permute-done | bytes 2592 | tf_op jit(solution)/shard_map/ppermute | solution.py:26
  55.4 6.8 collective-permute-done.7
  64.6 4.5 collective-permute-start.11
  71.5 10.8 %collective-permute-done.8 = f32[64,8,1]{2,1,0:T(8,128)S(1)} collective-permute-done((f32[64,8,1]{2,1,0:T(8,128)S(1)}, f32[64,8,1]{2,1,0:T(8,128)S(1)}, u32[]{:S(2)}, u32[]{:S(2)}) %collective-permute-start.8) | collective-permute-done | bytes 2080 | tf_op jit(solution)/shard_map/ppermute | solution.py:27
  90.0 3.5 collective-permute-start.15
  93.5 12.5 %collective-permute-done.14 = f32[64,10,1]{2,1,0:T(8,128)S(1)} collective-permute-done((f32[64,10,1]{2,1,0:T(8,128)S(1)}, f32[64,10,1]{2,1,0:T(8,128)S(1)}, u32[]{:S(2)}, u32[]{:S(2)}) %collective-permute-start.14) | collective-permute-done | bytes 2592 | tf_op jit(solution)/shard_map/ppermute | solution.py:26
  106.0 5.6 collective-permute-done.15
  114.0 4.5 collective-permute-start.19
  118.7 3.0 collective-permute-start.16
  121.7 10.4 %collective-permute-done.16 = f32[64,8,1]{2,1,0:T(8,128)S(1)} collective-permute-done((f32[64,8,1]{2,1,0:T(8,128)S(1)}, f32[64,8,1]{2,1,0:T(8,128)S(1)}, u32[]{:S(2)}, u32[]{:S(2)}) %collective-permute-start.16) | collective-permute-done | bytes 2080 | tf_op jit(solution)/shard_map/ppermute | solution.py:27
  140.3 3.3 collective-permute-start.23
  144.3 4.1 all-to-all-start.1
  148.4 8.0 %collective-permute-done.22 = f32[64,10,1]{2,1,0:T(8,128)S(1)} collective-permute-done((f32[64,10,1]{2,1,0:T(8,128)}, f32[64,10,1]{2,1,0:T(8,128)S(1)}, u32[]{:S(2)}, u32[]{:S(2)}) %collective-permute-start.22) | collective-permute-done | bytes 2592 | tf_op jit(solution)/shard_map/ppermute | solution.py:26
  156.3 5.7 collective-permute-done.23
  164.3 2.9 collective-permute-start.24
  168.5 4.5 collective-permute-start.27
  173.1 5.0 collective-permute-done.24
  184.9 3.2 collective-permute-start.31
  188.7 12.2 %collective-permute-done.30 = f32[64,10,1]{2,1,0:T(8,128)S(1)} collective-permute-done((f32[64,10,1]{2,1,0:T(8,128)S(1)}, f32[64,10,1]{2,1,0:T(8,128)S(1)}, u32[]{:S(2)}, u32[]{:S(2)}) %collective-permute-start.30) | collective-permute-done | bytes 2592 | tf_op jit(solution)/shard_map/ppermute | solution.py:26
  200.8 6.1 collective-permute-done.31
  211.7 4.5 collective-permute-start.35
  216.2 5.8 collective-permute-done.32
  230.0 3.3 collective-permute-start.39
  233.2 4.1 all-to-all-start
  238.8 7.4 collective-permute-done.38
  246.2 6.6 collective-permute-done.39
  259.1 5.2 collective-permute-start.43
  265.7 3.2 collective-permute-done.40
  277.2 34.1 %all-reduce.11.cloned.1.call-done = (f32[128,128]{1,0:T(8,128)}, f32[128,128]{0,1:T(8,128)}) async-done(((f32[128,128]{1,0:T(8,128)}, f32[128,128]{0,1:T(8,128)}), (f32[128,128]{1,0:T(8,128)}, f32[128,128]{0,1:T(8,128)})) %all-reduce.11.cloned.1.call-update) | async-done | bytes 131088 | tf_op jit(solution)/shard_map/psum | solution.py:16
  312.0 44.3 %all-reduce.15.cloned.1.call-done = (f32[128,128]{1,0:T(8,128)}, f32[128,128]{0,1:T(8,128)}) async-done(((f32[128,128]{1,0:T(8,128)}, f32[128,128]{0,1:T(8,128)}), (f32[128,128]{1,0:T(8,128)}, f32[128,128]{0,1:T(8,128)})) %all-reduce.15.cloned.1.call-update) | async-done | bytes 131088 | tf_op jit(solution)/shard_map/psum | solution.py:16
  358.0 11.7 %cholesky.44 = f32[128,128]{1,0:T(8,128)S(1)} custom-call(f32[128,128]{1,0:T(8,128)S(1)} %fusion.151), custom_call_target="Cholesky" | custom-call | tf_op jit(solution)/shard_map/jit(cholesky)/cholesky | solution.py:89
  371.1 9.8 %custom-call.8 = f32[1,128,128]{1,2,0:T(8,128)S(1)} custom-call(f32[1,128,128]{2,1,0:T(8,128)S(1)} %fusion.135), custom_call_target="InvertDiagBlocksLowerTriangular" | custom-call | tf_op jit(solution)/shard_map/jit(_cho_solve)/triangular_solve | solution.py:90
  394.7 12.8 %collective-permute-done.46 = f32[64,10,1]{2,1,0:T(8,128)S(1)} collective-permute-done((f32[64,10,1]{2,1,0:T(8,128)S(1)}, f32[64,10,1]{2,1,0:T(8,128)S(1)}, u32[]{:S(2)}, u32[]{:S(2)}) %collective-permute-start.46) | collective-permute-done | bytes 2592 | tf_op jit(solution)/shard_map/ppermute | solution.py:26
  407.5 7.6 %collective-permute-done.47 = f32[64,10,1]{2,1,0:T(8,128)S(1)} collective-permute-done((f32[64,10,1]{2,1,0:T(8,128)S(1)}, f32[64,10,1]{2,1,0:T(8,128)S(1)}, u32[]{:S(2)}, u32[]{:S(2)}) %collective-permute-start.47) | collective-permute-done | bytes 2592 | tf_op jit(solution)/shard_map/ppermute | solution.py:27
  417.5 4.8 collective-permute-start.51
  424.7 7.4 collective-permute-done.48
  432.0 3.7 collective-permute-done.49
  447.3 12.6 %collective-permute-done.54 = f32[64,10,1]{2,1,0:T(8,128)S(1)} collective-permute-done((f32[64,10,1]{2,1,0:T(8,128)S(1)}, f32[64,10,1]{2,1,0:T(8,128)S(1)}, u32[]{:S(2)}, u32[]{:S(2)}) %collective-permute-start.54) | collective-permute-done | bytes 2592 | tf_op jit(solution)/shard_map/ppermute | solution.py:26
  459.9 6.5 collective-permute-done.55
  468.8 4.5 collective-permute-start.59
  476.0 7.2 collective-permute-done.56
  483.1 3.4 collective-permute-done.57
  497.2 12.8 %collective-permute-done.62 = f32[64,10,1]{2,1,0:T(8,128)S(1)} collective-permute-done((f32[64,10,1]{2,1,0:T(8,128)S(1)}, f32[64,10,1]{2,1,0:T(8,128)S(1)}, u32[]{:S(2)}, u32[]{:S(2)}) %collective-permute-start.62) | collective-permute-done | bytes 2592 | tf_op jit(solution)/shard_map/ppermute | solution.py:26
  510.0 4.9 collective-permute-done.63
  517.4 4.5 collective-permute-start.67
  522.1 3.4 collective-permute-start.64
  525.4 7.2 collective-permute-done.64
  532.6 3.5 collective-permute-done.65
  546.8 12.8 %collective-permute-done.70 = f32[64,10,1]{2,1,0:T(8,128)S(1)} collective-permute-done((f32[64,10,1]{2,1,0:T(8,128)S(1)}, f32[64,10,1]{2,1,0:T(8,128)S(1)}, u32[]{:S(2)}, u32[]{:S(2)}) %collective-permute-start.70) | collective-permute-done | bytes 2592 | tf_op jit(solution)/shard_map/ppermute | solution.py:26
  559.6 4.5 collective-permute-done.71
  566.6 4.5 collective-permute-start.75
  573.3 9.5 %collective-permute-done.72 = f32[64,8,1]{2,1,0:T(8,128)S(1)} collective-permute-done((f32[64,8,1]{2,1,0:T(8,128)S(1)}, f32[64,8,1]{2,1,0:T(8,128)S(1)}, u32[]{:S(2)}, u32[]{:S(2)}) %collective-permute-start.72) | collective-permute-done | bytes 2080 | tf_op jit(solution)/shard_map/ppermute | solution.py:27
  593.8 12.6 %collective-permute-done.78 = f32[64,10,1]{2,1,0:T(8,128)S(1)} collective-permute-done((f32[64,10,1]{2,1,0:T(8,128)S(1)}, f32[64,10,1]{2,1,0:T(8,128)S(1)}, u32[]{:S(2)}, u32[]{:S(2)}) %collective-permute-start.78) | collective-permute-done | bytes 2592 | tf_op jit(solution)/shard_map/ppermute | solution.py:26
  606.4 5.4 collective-permute-done.79
  616.4 4.5 collective-permute-start.83
  621.3 5.5 collective-permute-done.80
  634.2 33.8 %all-reduce.9.cloned.1.call-done = (f32[128,128]{1,0:T(8,128)}, f32[128,128]{0,1:T(8,128)}) async-done(((f32[128,128]{1,0:T(8,128)}, f32[128,128]{0,1:T(8,128)}), (f32[128,128]{1,0:T(8,128)}, f32[128,128]{0,1:T(8,128)})) %all-reduce.9.cloned.1.call-update) | async-done | bytes 131088 | tf_op jit(solution)/shard_map/psum | solution.py:16
  668.7 44.2 %all-reduce.13.cloned.1.call-done = (f32[128,128]{1,0:T(8,128)}, f32[128,128]{0,1:T(8,128)}) async-done(((f32[128,128]{1,0:T(8,128)}, f32[128,128]{0,1:T(8,128)}), (f32[128,128]{1,0:T(8,128)}, f32[128,128]{0,1:T(8,128)})) %all-reduce.13.cloned.1.call-update) | async-done | bytes 131088 | tf_op jit(solution)/shard_map/psum | solution.py:16
  714.6 11.7 %cholesky.55 = f32[128,128]{1,0:T(8,128)S(1)} custom-call(f32[128,128]{1,0:T(8,128)S(1)} %fusion.146), custom_call_target="Cholesky" | custom-call | tf_op jit(solution)/shard_map/jit(cholesky)/cholesky | solution.py:89
  727.6 9.8 %custom-call.9 = f32[1,128,128]{1,2,0:T(8,128)S(1)} custom-call(f32[1,128,128]{2,1,0:T(8,128)S(1)} %fusion.136), custom_call_target="InvertDiagBlocksLowerTriangular" | custom-call | tf_op jit(solution)/shard_map/jit(_cho_solve)/triangular_solve | solution.py:90
  (350 shorter events, 177.3 us)
Async XLA Ops:
  8.2 22.9 %collective-permute-start.2 = (f32[64,1,128]{2,1,0:T(1,128)S(1)}, f32[64,1,128]{2,1,0:T(1,128)S(1)}, u32[]{:S(2)}, u32[]{:S(2)}) collective-permute-start(f32[64,1,128]{2,1,0:T(1,128)S(1)} %broadcast_in_dim.82), channel_id=1, source_target_pairs={{8,0},{16,8},{24,16},{9,1},{17,9},{25,17},{10,2},{18,10},{26,18},{... | collective-permute-start | bytes 98312 | tf_op jit(solution)/shard_map/ppermute | solution.py:27
  9.5 21.5 %collective-permute-start.3 = (f32[64,1,128]{2,1,0:T(1,128)S(1)}, f32[64,1,128]{2,1,0:T(1,128)S(1)}, u32[]{:S(2)}, u32[]{:S(2)}) collective-permute-start(f32[64,1,128]{2,1,0:T(1,128)S(1)} %broadcast_in_dim.83), channel_id=1, source_target_pairs={{0,8},{8,16},{16,24},{1,9},{9,17},{17,25},{2,10},{10,18},{18,26},{... | collective-permute-start | bytes 98312 | tf_op jit(solution)/shard_map/ppermute | solution.py:26
  15.3 10.9 %collective-permute-start = (f32[64,8,1]{2,1,0:T(8,128)S(1)}, f32[64,8,1]{2,1,0:T(8,128)S(1)}, u32[]{:S(2)}, u32[]{:S(2)}) collective-permute-start(f32[64,8,1]{2,1,0:T(8,128)S(1)} %broadcast_in_dim.78), channel_id=1, source_target_pairs={{2,0},{4,2},{6,4},{0,6},{3,1},{5,3},{7,5},{1,7},{10,8},{12,10},{14... | collective-permute-start | bytes 6152 | tf_op jit(solution)/shard_map/ppermute | solution.py:27
  19.6 11.4 %collective-permute-start.1 = (f32[64,8,1]{2,1,0:T(8,128)S(1)}, f32[64,8,1]{2,1,0:T(8,128)S(1)}, u32[]{:S(2)}, u32[]{:S(2)}) collective-permute-start(f32[64,8,1]{2,1,0:T(8,128)S(1)} %broadcast_in_dim.79), channel_id=1, source_target_pairs={{0,2},{2,4},{4,6},{6,0},{1,3},{3,5},{5,7},{7,1},{8,10},{10,12},{12... | collective-permute-start | bytes 6152 | tf_op jit(solution)/shard_map/ppermute | solution.py:26
  38.7 16.6 %collective-permute-start.6 = (f32[64,10,1]{2,1,0:T(8,128)S(1)}, f32[64,10,1]{2,1,0:T(8,128)S(1)}, u32[]{:S(2)}, u32[]{:S(2)}) collective-permute-start(f32[64,10,1]{2,1,0:T(8,128)S(1)} %get-tuple-element.60), channel_id=1, source_target_pairs={{0,2},{2,4},{4,6},{6,0},{1,3},{3,5},{5,7},{7,1},{8,10},{10,12},{12... | collective-permute-start | bytes 7688 | tf_op jit(solution)/shard_map/ppermute | solution.py:26
  40.4 21.8 %collective-permute-start.7 = (f32[64,10,1]{2,1,0:T(8,128)S(1)}, f32[64,10,1]{2,1,0:T(8,128)S(1)}, u32[]{:S(2)}, u32[]{:S(2)}) collective-permute-start(f32[64,10,1]{2,1,0:T(8,128)S(1)} %get-tuple-element.61), channel_id=1, source_target_pairs={{2,0},{4,2},{6,4},{0,6},{3,1},{5,3},{7,5},{1,7},{10,8},{12,10},{14... | collective-permute-start | bytes 7688 | tf_op jit(solution)/shard_map/ppermute | solution.py:27
  63.3 18.9 %collective-permute-start.10 = (f32[64,1,128]{2,1,0:T(1,128)S(1)}, f32[64,1,128]{2,1,0:T(1,128)S(1)}, u32[]{:S(2)}, u32[]{:S(2)}) collective-permute-start(f32[64,1,128]{2,1,0:T(1,128)S(1)} %get-tuple-element.118), channel_id=1, source_target_pairs={{8,0},{16,8},{24,16},{9,1},{17,9},{25,17},{10,2},{18,10},{26,18},{... | collective-permute-start | bytes 98312 | tf_op jit(solution)/shard_map/ppermute | solution.py:27
  64.6 17.6 %collective-permute-start.11 = (f32[64,1,128]{2,1,0:T(1,128)S(1)}, f32[64,1,128]{2,1,0:T(1,128)S(1)}, u32[]{:S(2)}, u32[]{:S(2)}) collective-permute-start(f32[64,1,128]{2,1,0:T(1,128)S(1)} %get-tuple-element.119), channel_id=1, source_target_pairs={{0,8},{8,16},{16,24},{1,9},{9,17},{17,25},{2,10},{10,18},{18,26},{... | collective-permute-start | bytes 98312 | tf_op jit(solution)/shard_map/ppermute | solution.py:26
  69.3 12.9 %collective-permute-start.8 = (f32[64,8,1]{2,1,0:T(8,128)S(1)}, f32[64,8,1]{2,1,0:T(8,128)S(1)}, u32[]{:S(2)}, u32[]{:S(2)}) collective-permute-start(f32[64,8,1]{2,1,0:T(8,128)S(1)} %get-tuple-element.116), channel_id=1, source_target_pairs={{2,0},{4,2},{6,4},{0,6},{3,1},{5,3},{7,5},{1,7},{10,8},{12,10},{14... | collective-permute-start | bytes 6152 | tf_op jit(solution)/shard_map/ppermute | solution.py:27
  71.4 10.8 %collective-permute-start.9 = (f32[64,8,1]{2,1,0:T(8,128)S(1)}, f32[64,8,1]{2,1,0:T(8,128)S(1)}, u32[]{:S(2)}, u32[]{:S(2)}) collective-permute-start(f32[64,8,1]{2,1,0:T(8,128)S(1)} %get-tuple-element.117), channel_id=1, source_target_pairs={{0,2},{2,4},{4,6},{6,0},{1,3},{3,5},{5,7},{7,1},{8,10},{10,12},{12... | collective-permute-start | bytes 6152 | tf_op jit(solution)/shard_map/ppermute | solution.py:26
  89.7 16.4 %collective-permute-start.14 = (f32[64,10,1]{2,1,0:T(8,128)S(1)}, f32[64,10,1]{2,1,0:T(8,128)S(1)}, u32[]{:S(2)}, u32[]{:S(2)}) collective-permute-start(f32[64,10,1]{2,1,0:T(8,128)S(1)} %get-tuple-element.58), channel_id=1, source_target_pairs={{0,2},{2,4},{4,6},{6,0},{1,3},{3,5},{5,7},{7,1},{8,10},{10,12},{12... | collective-permute-start | bytes 7688 | tf_op jit(solution)/shard_map/ppermute | solution.py:26
  90.0 21.6 %collective-permute-start.15 = (f32[64,10,1]{2,1,0:T(8,128)S(1)}, f32[64,10,1]{2,1,0:T(8,128)S(1)}, u32[]{:S(2)}, u32[]{:S(2)}) collective-permute-start(f32[64,10,1]{2,1,0:T(8,128)S(1)} %get-tuple-element.59), channel_id=1, source_target_pairs={{2,0},{4,2},{6,4},{0,6},{3,1},{5,3},{7,5},{1,7},{10,8},{12,10},{14... | collective-permute-start | bytes 7688 | tf_op jit(solution)/shard_map/ppermute | solution.py:27
  112.7 19.3 %collective-permute-start.18 = (f32[64,1,128]{2,1,0:T(1,128)S(1)}, f32[64,1,128]{2,1,0:T(1,128)S(1)}, u32[]{:S(2)}, u32[]{:S(2)}) collective-permute-start(f32[64,1,128]{2,1,0:T(1,128)S(1)} %get-tuple-element.112), channel_id=1, source_target_pairs={{8,0},{16,8},{24,16},{9,1},{17,9},{25,17},{10,2},{18,10},{26,18},{... | collective-permute-start | bytes 98312 | tf_op jit(solution)/shard_map/ppermute | solution.py:27
  114.0 18.0 %collective-permute-start.19 = (f32[64,1,128]{2,1,0:T(1,128)S(1)}, f32[64,1,128]{2,1,0:T(1,128)S(1)}, u32[]{:S(2)}, u32[]{:S(2)}) collective-permute-start(f32[64,1,128]{2,1,0:T(1,128)S(1)} %get-tuple-element.113), channel_id=1, source_target_pairs={{0,8},{8,16},{16,24},{1,9},{9,17},{17,25},{2,10},{10,18},{18,26},{... | collective-permute-start | bytes 98312 | tf_op jit(solution)/shard_map/ppermute | solution.py:26
  118.7 13.3 %collective-permute-start.16 = (f32[64,8,1]{2,1,0:T(8,128)S(1)}, f32[64,8,1]{2,1,0:T(8,128)S(1)}, u32[]{:S(2)}, u32[]{:S(2)}) collective-permute-start(f32[64,8,1]{2,1,0:T(8,128)S(1)} %get-tuple-element.110), channel_id=1, source_target_pairs={{2,0},{4,2},{6,4},{0,6},{3,1},{5,3},{7,5},{1,7},{10,8},{12,10},{14... | collective-permute-start | bytes 6152 | tf_op jit(solution)/shard_map/ppermute | solution.py:27
  139.8 16.6 %collective-permute-start.22 = (f32[64,10,1]{2,1,0:T(8,128)}, f32[64,10,1]{2,1,0:T(8,128)S(1)}, u32[]{:S(2)}, u32[]{:S(2)}) collective-permute-start(f32[64,10,1]{2,1,0:T(8,128)} %get-tuple-element.56), channel_id=1, source_target_pairs={{0,2},{2,4},{4,6},{6,0},{1,3},{3,5},{5,7},{7,1},{8,10},{10,12},{12... | collective-permute-start | bytes 7688 | tf_op jit(solution)/shard_map/ppermute | solution.py:26
  140.3 21.7 %collective-permute-start.23 = (f32[64,10,1]{2,1,0:T(8,128)}, f32[64,10,1]{2,1,0:T(8,128)}, u32[]{:S(2)}, u32[]{:S(2)}) collective-permute-start(f32[64,10,1]{2,1,0:T(8,128)} %get-tuple-element.57), channel_id=1, source_target_pairs={{2,0},{4,2},{6,4},{0,6},{3,1},{5,3},{7,5},{1,7},{10,8},{12,10},{14... | collective-permute-start | bytes 7688 | tf_op jit(solution)/shard_map/ppermute | solution.py:27
  144.3 89.0 %all-to-all-start.1 = ((f32[2,16,8]{2,0,1:T(2,128)}), f32[2,16,8]{2,0,1:T(2,128)}, u32[]{:S(2)}, u32[]{:S(2)}) async-start(f32[2,16,8]{2,0,1:T(2,128)} %bitcast.16), calls=%async_computation.1 | async-start | bytes 32768 | tf_op jit(solution)/shard_map/all_to_all | solution.py:100
  164.3 13.8 %collective-permute-start.24 = (f32[64,8,1]{2,1,0:T(8,128)S(1)}, f32[64,8,1]{2,1,0:T(8,128)S(1)}, u32[]{:S(2)}, u32[]{:S(2)}) collective-permute-start(f32[64,8,1]{2,1,0:T(8,128)S(1)} %get-tuple-element.104), channel_id=1, source_target_pairs={{2,0},{4,2},{6,4},{0,6},{3,1},{5,3},{7,5},{1,7},{10,8},{12,10},{14... | collective-permute-start | bytes 6152 | tf_op jit(solution)/shard_map/ppermute | solution.py:27
  167.2 10.9 %collective-permute-start.25 = (f32[64,8,1]{2,1,0:T(8,128)S(1)}, f32[64,8,1]{2,1,0:T(8,128)S(1)}, u32[]{:S(2)}, u32[]{:S(2)}) collective-permute-start(f32[64,8,1]{2,1,0:T(8,128)S(1)} %get-tuple-element.105), channel_id=1, source_target_pairs={{0,2},{2,4},{4,6},{6,0},{1,3},{3,5},{5,7},{7,1},{8,10},{10,12},{12... | collective-permute-start | bytes 6152 | tf_op jit(solution)/shard_map/ppermute | solution.py:26
  167.2 10.9 %collective-permute-start.26 = (f32[64,1,128]{2,1,0:T(1,128)S(1)}, f32[64,1,128]{2,1,0:T(1,128)S(1)}, u32[]{:S(2)}, u32[]{:S(2)}) collective-permute-start(f32[64,1,128]{2,1,0:T(1,128)S(1)} %get-tuple-element.106), channel_id=1, source_target_pairs={{8,0},{16,8},{24,16},{9,1},{17,9},{25,17},{10,2},{18,10},{26,18},{... | collective-permute-start | bytes 98312 | tf_op jit(solution)/shard_map/ppermute | solution.py:27
  184.2 16.6 %collective-permute-start.30 = (f32[64,10,1]{2,1,0:T(8,128)S(1)}, f32[64,10,1]{2,1,0:T(8,128)S(1)}, u32[]{:S(2)}, u32[]{:S(2)}) collective-permute-start(f32[64,10,1]{2,1,0:T(8,128)S(1)} %get-tuple-element.54), channel_id=1, source_target_pairs={{0,2},{2,4},{4,6},{6,0},{1,3},{3,5},{5,7},{7,1},{8,10},{10,12},{12... | collective-permute-start | bytes 7688 | tf_op jit(solution)/shard_map/ppermute | solution.py:26
  184.9 22.1 %collective-permute-start.31 = (f32[64,10,1]{2,1,0:T(8,128)S(1)}, f32[64,10,1]{2,1,0:T(8,128)S(1)}, u32[]{:S(2)}, u32[]{:S(2)}) collective-permute-start(f32[64,10,1]{2,1,0:T(8,128)S(1)} %get-tuple-element.55), channel_id=1, source_target_pairs={{2,0},{4,2},{6,4},{0,6},{3,1},{5,3},{7,5},{1,7},{10,8},{12,10},{14... | collective-permute-start | bytes 7688 | tf_op jit(solution)/shard_map/ppermute | solution.py:27
  208.2 13.9 %collective-permute-start.32 = (f32[64,8,1]{2,1,0:T(8,128)S(1)}, f32[64,8,1]{2,1,0:T(8,128)S(1)}, u32[]{:S(2)}, u32[]{:S(2)}) collective-permute-start(f32[64,8,1]{2,1,0:T(8,128)S(1)} %get-tuple-element.98), channel_id=1, source_target_pairs={{2,0},{4,2},{6,4},{0,6},{3,1},{5,3},{7,5},{1,7},{10,8},{12,10},{14... | collective-permute-start | bytes 6152 | tf_op jit(solution)/shard_map/ppermute | solution.py:27
  210.3 11.8 %collective-permute-start.33 = (f32[64,8,1]{2,1,0:T(8,128)S(1)}, f32[64,8,1]{2,1,0:T(8,128)S(1)}, u32[]{:S(2)}, u32[]{:S(2)}) collective-permute-start(f32[64,8,1]{2,1,0:T(8,128)S(1)} %get-tuple-element.99), channel_id=1, source_target_pairs={{0,2},{2,4},{4,6},{6,0},{1,3},{3,5},{5,7},{7,1},{8,10},{10,12},{12... | collective-permute-start | bytes 6152 | tf_op jit(solution)/shard_map/ppermute | solution.py:26
  210.4 11.7 %collective-permute-start.34 = (f32[64,1,128]{2,1,0:T(1,128)S(1)}, f32[64,1,128]{2,1,0:T(1,128)S(1)}, u32[]{:S(2)}, u32[]{:S(2)}) collective-permute-start(f32[64,1,128]{2,1,0:T(1,128)S(1)} %get-tuple-element.100), channel_id=1, source_target_pairs={{8,0},{16,8},{24,16},{9,1},{17,9},{25,17},{10,2},{18,10},{26,18},{... | collective-permute-start | bytes 98312 | tf_op jit(solution)/shard_map/ppermute | solution.py:27
  229.4 16.8 %collective-permute-start.38 = (f32[64,10,1]{2,1,0:T(8,128)}, f32[64,10,1]{2,1,0:T(8,128)S(1)}, u32[]{:S(2)}, u32[]{:S(2)}) collective-permute-start(f32[64,10,1]{2,1,0:T(8,128)} %get-tuple-element.52), channel_id=1, source_target_pairs={{0,2},{2,4},{4,6},{6,0},{1,3},{3,5},{5,7},{7,1},{8,10},{10,12},{12... | collective-permute-start | bytes 7688 | tf_op jit(solution)/shard_map/ppermute | solution.py:26
  230.0 22.8 %collective-permute-start.39 = (f32[64,10,1]{2,1,0:T(8,128)S(1)}, f32[64,10,1]{2,1,0:T(8,128)}, u32[]{:S(2)}, u32[]{:S(2)}) collective-permute-start(f32[64,10,1]{2,1,0:T(8,128)S(1)} %get-tuple-element.53), channel_id=1, source_target_pairs={{2,0},{4,2},{6,4},{0,6},{3,1},{5,3},{7,5},{1,7},{10,8},{12,10},{14... | collective-permute-start | bytes 7688 | tf_op jit(solution)/shard_map/ppermute | solution.py:27
  233.2 31.0 %all-to-all-start = ((f32[2,16,8]{2,0,1:T(2,128)}), f32[2,16,8]{2,0,1:T(2,128)}, u32[]{:S(2)}, u32[]{:S(2)}) async-start(f32[2,16,8]{2,0,1:T(2,128)} %bitcast.208), calls=%async_computation | async-start | bytes 32768 | tf_op jit(solution)/shard_map/all_to_all | solution.py:101
  237.3 74.1 %all-reduce.11.cloned.1.call-start = ((), (), s32[]{:S(2)}) async-start(), calls=%async_computation.5 | async-start | bytes 262144 | tf_op jit(solution)/shard_map/psum | solution.py:16
  255.0 13.8 %collective-permute-start.40 = (f32[64,8,1]{2,1,0:T(8,128)S(1)}, f32[64,8,1]{2,1,0:T(8,128)S(1)}, u32[]{:S(2)}, u32[]{:S(2)}) collective-permute-start(f32[64,8,1]{2,1,0:T(8,128)S(1)} %get-tuple-element.92), channel_id=1, source_target_pairs={{2,0},{4,2},{6,4},{0,6},{3,1},{5,3},{7,5},{1,7},{10,8},{12,10},{14... | collective-permute-start | bytes 6152 | tf_op jit(solution)/shard_map/ppermute | solution.py:27
  257.1 11.7 %collective-permute-start.41 = (f32[64,8,1]{2,1,0:T(8,128)S(1)}, f32[64,8,1]{2,1,0:T(8,128)S(1)}, u32[]{:S(2)}, u32[]{:S(2)}) collective-permute-start(f32[64,8,1]{2,1,0:T(8,128)S(1)} %get-tuple-element.93), channel_id=1, source_target_pairs={{0,2},{2,4},{4,6},{6,0},{1,3},{3,5},{5,7},{7,1},{8,10},{10,12},{12... | collective-permute-start | bytes 6152 | tf_op jit(solution)/shard_map/ppermute | solution.py:26
  257.8 11.1 %collective-permute-start.42 = (f32[64,1,128]{2,1,0:T(1,128)}, f32[64,1,128]{2,1,0:T(1,128)}, u32[]{:S(2)}, u32[]{:S(2)}) collective-permute-start(f32[64,1,128]{2,1,0:T(1,128)} %get-tuple-element.94), channel_id=1, source_target_pairs={{8,0},{16,8},{24,16},{9,1},{17,9},{25,17},{10,2},{18,10},{26,18},{... | collective-permute-start | bytes 98312 | tf_op jit(solution)/shard_map/ppermute | solution.py:27
  277.2 79.1 %all-reduce.15.cloned.1.call-start = ((), (), s32[]{:S(2)}) async-start(), calls=%async_computation.7 | async-start | bytes 262144 | tf_op jit(solution)/shard_map/psum | solution.py:16
  311.4 70.1 %all-gather.3.cloned.1.call-start = ((), (), s32[]{:S(2)}) async-start(), calls=%async_computation.2 | async-start | bytes 1572864 | tf_op jit(solution)/shard_map/all_gather | solution.py:125
  312.0 356.1 %all-reduce.9.cloned.1.call-start = ((), (), s32[]{:S(2)}) async-start(), calls=%async_computation.4 | async-start | bytes 262144 | tf_op jit(solution)/shard_map/psum | solution.py:16
  390.8 16.7 %collective-permute-start.46 = (f32[64,10,1]{2,1,0:T(8,128)S(1)}, f32[64,10,1]{2,1,0:T(8,128)S(1)}, u32[]{:S(2)}, u32[]{:S(2)}) collective-permute-start(f32[64,10,1]{2,1,0:T(8,128)S(1)} %get-tuple-element.48), channel_id=1, source_target_pairs={{0,2},{2,4},{4,6},{6,0},{1,3},{3,5},{5,7},{7,1},{8,10},{10,12},{12... | collective-permute-start | bytes 7688 | tf_op jit(solution)/shard_map/ppermute | solution.py:26
  392.4 22.7 %collective-permute-start.47 = (f32[64,10,1]{2,1,0:T(8,128)S(1)}, f32[64,10,1]{2,1,0:T(8,128)S(1)}, u32[]{:S(2)}, u32[]{:S(2)}) collective-permute-start(f32[64,10,1]{2,1,0:T(8,128)S(1)} %get-tuple-element.49), channel_id=1, source_target_pairs={{2,0},{4,2},{6,4},{0,6},{3,1},{5,3},{7,5},{1,7},{10,8},{12,10},{14... | collective-permute-start | bytes 7688 | tf_op jit(solution)/shard_map/ppermute | solution.py:27
  416.2 19.6 %collective-permute-start.50 = (f32[64,1,128]{2,1,0:T(1,128)S(1)}, f32[64,1,128]{2,1,0:T(1,128)S(1)}, u32[]{:S(2)}, u32[]{:S(2)}) collective-permute-start(f32[64,1,128]{2,1,0:T(1,128)S(1)} %get-tuple-element.88), channel_id=1, source_target_pairs={{8,0},{16,8},{24,16},{9,1},{17,9},{25,17},{10,2},{18,10},{26,18},{... | collective-permute-start | bytes 98312 | tf_op jit(solution)/shard_map/ppermute | solution.py:27
  417.5 18.3 %collective-permute-start.51 = (f32[64,1,128]{2,1,0:T(1,128)S(1)}, f32[64,1,128]{2,1,0:T(1,128)S(1)}, u32[]{:S(2)}, u32[]{:S(2)}) collective-permute-start(f32[64,1,128]{2,1,0:T(1,128)S(1)} %get-tuple-element.89), channel_id=1, source_target_pairs={{0,8},{8,16},{16,24},{1,9},{9,17},{17,25},{2,10},{10,18},{18,26},{... | collective-permute-start | bytes 98312 | tf_op jit(solution)/shard_map/ppermute | solution.py:26
  424.7 11.1 %collective-permute-start.49 = (f32[64,8,1]{2,1,0:T(8,128)S(1)}, f32[64,8,1]{2,1,0:T(8,128)S(1)}, u32[]{:S(2)}, u32[]{:S(2)}) collective-permute-start(f32[64,8,1]{2,1,0:T(8,128)S(1)} %get-tuple-element.87), channel_id=1, source_target_pairs={{0,2},{2,4},{4,6},{6,0},{1,3},{3,5},{5,7},{7,1},{8,10},{10,12},{12... | collective-permute-start | bytes 6152 | tf_op jit(solution)/shard_map/ppermute | solution.py:26
  443.3 16.6 %collective-permute-start.54 = (f32[64,10,1]{2,1,0:T(8,128)S(1)}, f32[64,10,1]{2,1,0:T(8,128)S(1)}, u32[]{:S(2)}, u32[]{:S(2)}) collective-permute-start(f32[64,10,1]{2,1,0:T(8,128)S(1)} %get-tuple-element.46), channel_id=1, source_target_pairs={{0,2},{2,4},{4,6},{6,0},{1,3},{3,5},{5,7},{7,1},{8,10},{10,12},{12... | collective-permute-start | bytes 7688 | tf_op jit(solution)/shard_map/ppermute | solution.py:26
  444.8 21.6 %collective-permute-start.55 = (f32[64,10,1]{2,1,0:T(8,128)S(1)}, f32[64,10,1]{2,1,0:T(8,128)S(1)}, u32[]{:S(2)}, u32[]{:S(2)}) collective-permute-start(f32[64,10,1]{2,1,0:T(8,128)S(1)} %get-tuple-element.47), channel_id=1, source_target_pairs={{2,0},{4,2},{6,4},{0,6},{3,1},{5,3},{7,5},{1,7},{10,8},{12,10},{14... | collective-permute-start | bytes 7688 | tf_op jit(solution)/shard_map/ppermute | solution.py:27
  467.5 19.0 %collective-permute-start.58 = (f32[64,1,128]{2,1,0:T(1,128)S(1)}, f32[64,1,128]{2,1,0:T(1,128)S(1)}, u32[]{:S(2)}, u32[]{:S(2)}) collective-permute-start(f32[64,1,128]{2,1,0:T(1,128)S(1)} %get-tuple-element.82), channel_id=1, source_target_pairs={{8,0},{16,8},{24,16},{9,1},{17,9},{25,17},{10,2},{18,10},{26,18},{... | collective-permute-start | bytes 98312 | tf_op jit(solution)/shard_map/ppermute | solution.py:27
  468.8 17.8 %collective-permute-start.59 = (f32[64,1,128]{2,1,0:T(1,128)S(1)}, f32[64,1,128]{2,1,0:T(1,128)S(1)}, u32[]{:S(2)}, u32[]{:S(2)}) collective-permute-start(f32[64,1,128]{2,1,0:T(1,128)S(1)} %get-tuple-element.83), channel_id=1, source_target_pairs={{0,8},{8,16},{16,24},{1,9},{9,17},{17,25},{2,10},{10,18},{18,26},{... | collective-permute-start | bytes 98312 | tf_op jit(solution)/shard_map/ppermute | solution.py:26
  476.0 10.6 %collective-permute-start.57 = (f32[64,8,1]{2,1,0:T(8,128)S(1)}, f32[64,8,1]{2,1,0:T(8,128)S(1)}, u32[]{:S(2)}, u32[]{:S(2)}) collective-permute-start(f32[64,8,1]{2,1,0:T(8,128)S(1)} %get-tuple-element.81), channel_id=1, source_target_pairs={{0,2},{2,4},{4,6},{6,0},{1,3},{3,5},{5,7},{7,1},{8,10},{10,12},{12... | collective-permute-start | bytes 6152 | tf_op jit(solution)/shard_map/ppermute | solution.py:26
  493.4 16.6 %collective-permute-start.62 = (f32[64,10,1]{2,1,0:T(8,128)S(1)}, f32[64,10,1]{2,1,0:T(8,128)S(1)}, u32[]{:S(2)}, u32[]{:S(2)}) collective-permute-start(f32[64,10,1]{2,1,0:T(8,128)S(1)} %get-tuple-element.44), channel_id=1, source_target_pairs={{0,2},{2,4},{4,6},{6,0},{1,3},{3,5},{5,7},{7,1},{8,10},{10,12},{12... | collective-permute-start | bytes 7688 | tf_op jit(solution)/shard_map/ppermute | solution.py:26
  494.9 20.0 %collective-permute-start.63 = (f32[64,10,1]{2,1,0:T(8,128)S(1)}, f32[64,10,1]{2,1,0:T(8,128)S(1)}, u32[]{:S(2)}, u32[]{:S(2)}) collective-permute-start(f32[64,10,1]{2,1,0:T(8,128)S(1)} %get-tuple-element.45), channel_id=1, source_target_pairs={{2,0},{4,2},{6,4},{0,6},{3,1},{5,3},{7,5},{1,7},{10,8},{12,10},{14... | collective-permute-start | bytes 7688 | tf_op jit(solution)/shard_map/ppermute | solution.py:27
  516.1 20.0 %collective-permute-start.66 = (f32[64,1,128]{2,1,0:T(1,128)S(1)}, f32[64,1,128]{2,1,0:T(1,128)S(1)}, u32[]{:S(2)}, u32[]{:S(2)}) collective-permute-start(f32[64,1,128]{2,1,0:T(1,128)S(1)} %get-tuple-element.76), channel_id=1, source_target_pairs={{8,0},{16,8},{24,16},{9,1},{17,9},{25,17},{10,2},{18,10},{26,18},{... | collective-permute-start | bytes 98312 | tf_op jit(solution)/shard_map/ppermute | solution.py:27
  517.4 18.7 %collective-permute-start.67 = (f32[64,1,128]{2,1,0:T(1,128)S(1)}, f32[64,1,128]{2,1,0:T(1,128)S(1)}, u32[]{:S(2)}, u32[]{:S(2)}) collective-permute-start(f32[64,1,128]{2,1,0:T(1,128)S(1)} %get-tuple-element.77), channel_id=1, source_target_pairs={{0,8},{8,16},{16,24},{1,9},{9,17},{17,25},{2,10},{10,18},{18,26},{... | collective-permute-start | bytes 98312 | tf_op jit(solution)/shard_map/ppermute | solution.py:26
  522.1 10.5 %collective-permute-start.64 = (f32[64,8,1]{2,1,0:T(8,128)S(1)}, f32[64,8,1]{2,1,0:T(8,128)S(1)}, u32[]{:S(2)}, u32[]{:S(2)}) collective-permute-start(f32[64,8,1]{2,1,0:T(8,128)S(1)} %get-tuple-element.74), channel_id=1, source_target_pairs={{2,0},{4,2},{6,4},{0,6},{3,1},{5,3},{7,5},{1,7},{10,8},{12,10},{14... | collective-permute-start | bytes 6152 | tf_op jit(solution)/shard_map/ppermute | solution.py:27
  525.4 10.6 %collective-permute-start.65 = (f32[64,8,1]{2,1,0:T(8,128)S(1)}, f32[64,8,1]{2,1,0:T(8,128)S(1)}, u32[]{:S(2)}, u32[]{:S(2)}) collective-permute-start(f32[64,8,1]{2,1,0:T(8,128)S(1)} %get-tuple-element.75), channel_id=1, source_target_pairs={{0,2},{2,4},{4,6},{6,0},{1,3},{3,5},{5,7},{7,1},{8,10},{10,12},{12... | collective-permute-start | bytes 6152 | tf_op jit(solution)/shard_map/ppermute | solution.py:26
  543.0 16.6 %collective-permute-start.70 = (f32[64,10,1]{2,1,0:T(8,128)S(1)}, f32[64,10,1]{2,1,0:T(8,128)S(1)}, u32[]{:S(2)}, u32[]{:S(2)}) collective-permute-start(f32[64,10,1]{2,1,0:T(8,128)S(1)} %get-tuple-element.42), channel_id=1, source_target_pairs={{0,2},{2,4},{4,6},{6,0},{1,3},{3,5},{5,7},{7,1},{8,10},{10,12},{12... | collective-permute-start | bytes 7688 | tf_op jit(solution)/shard_map/ppermute | solution.py:26
  544.5 19.6 %collective-permute-start.71 = (f32[64,10,1]{2,1,0:T(8,128)S(1)}, f32[64,10,1]{2,1,0:T(8,128)S(1)}, u32[]{:S(2)}, u32[]{:S(2)}) collective-permute-start(f32[64,10,1]{2,1,0:T(8,128)S(1)} %get-tuple-element.43), channel_id=1, source_target_pairs={{2,0},{4,2},{6,4},{0,6},{3,1},{5,3},{7,5},{1,7},{10,8},{12,10},{14... | collective-permute-start | bytes 7688 | tf_op jit(solution)/shard_map/ppermute | solution.py:27
  565.3 17.6 %collective-permute-start.74 = (f32[64,1,128]{2,1,0:T(1,128)S(1)}, f32[64,1,128]{2,1,0:T(1,128)S(1)}, u32[]{:S(2)}, u32[]{:S(2)}) collective-permute-start(f32[64,1,128]{2,1,0:T(1,128)S(1)} %get-tuple-element.70), channel_id=1, source_target_pairs={{8,0},{16,8},{24,16},{9,1},{17,9},{25,17},{10,2},{18,10},{26,18},{... | collective-permute-start | bytes 98312 | tf_op jit(solution)/shard_map/ppermute | solution.py:27
  566.6 16.3 %collective-permute-start.75 = (f32[64,1,128]{2,1,0:T(1,128)S(1)}, f32[64,1,128]{2,1,0:T(1,128)S(1)}, u32[]{:S(2)}, u32[]{:S(2)}) collective-permute-start(f32[64,1,128]{2,1,0:T(1,128)S(1)} %get-tuple-element.71), channel_id=1, source_target_pairs={{0,8},{8,16},{16,24},{1,9},{9,17},{17,25},{2,10},{10,18},{18,26},{... | collective-permute-start | bytes 98312 | tf_op jit(solution)/shard_map/ppermute | solution.py:26
  571.3 11.6 %collective-permute-start.72 = (f32[64,8,1]{2,1,0:T(8,128)S(1)}, f32[64,8,1]{2,1,0:T(8,128)S(1)}, u32[]{:S(2)}, u32[]{:S(2)}) collective-permute-start(f32[64,8,1]{2,1,0:T(8,128)S(1)} %get-tuple-element.68), channel_id=1, source_target_pairs={{2,0},{4,2},{6,4},{0,6},{3,1},{5,3},{7,5},{1,7},{10,8},{12,10},{14... | collective-permute-start | bytes 6152 | tf_op jit(solution)/shard_map/ppermute | solution.py:27
  589.9 16.4 %collective-permute-start.78 = (f32[64,10,1]{2,1,0:T(8,128)S(1)}, f32[64,10,1]{2,1,0:T(8,128)S(1)}, u32[]{:S(2)}, u32[]{:S(2)}) collective-permute-start(f32[64,10,1]{2,1,0:T(8,128)S(1)} %get-tuple-element.40), channel_id=1, source_target_pairs={{0,2},{2,4},{4,6},{6,0},{1,3},{3,5},{5,7},{7,1},{8,10},{10,12},{12... | collective-permute-start | bytes 7688 | tf_op jit(solution)/shard_map/ppermute | solution.py:26
  591.3 20.5 %collective-permute-start.79 = (f32[64,10,1]{2,1,0:T(8,128)S(1)}, f32[64,10,1]{2,1,0:T(8,128)S(1)}, u32[]{:S(2)}, u32[]{:S(2)}) collective-permute-start(f32[64,10,1]{2,1,0:T(8,128)S(1)} %get-tuple-element.41), channel_id=1, source_target_pairs={{2,0},{4,2},{6,4},{0,6},{3,1},{5,3},{7,5},{1,7},{10,8},{12,10},{14... | collective-permute-start | bytes 7688 | tf_op jit(solution)/shard_map/ppermute | solution.py:27
  613.0 13.7 %collective-permute-start.80 = (f32[64,8,1]{2,1,0:T(8,128)S(1)}, f32[64,8,1]{2,1,0:T(8,128)S(1)}, u32[]{:S(2)}, u32[]{:S(2)}) collective-permute-start(f32[64,8,1]{2,1,0:T(8,128)S(1)} %get-tuple-element.62), channel_id=1, source_target_pairs={{2,0},{4,2},{6,4},{0,6},{3,1},{5,3},{7,5},{1,7},{10,8},{12,10},{14... | collective-permute-start | bytes 6152 | tf_op jit(solution)/shard_map/ppermute | solution.py:27
  614.9 11.8 %collective-permute-start.81 = (f32[64,8,1]{2,1,0:T(8,128)S(1)}, f32[64,8,1]{2,1,0:T(8,128)S(1)}, u32[]{:S(2)}, u32[]{:S(2)}) collective-permute-start(f32[64,8,1]{2,1,0:T(8,128)S(1)} %get-tuple-element.63), channel_id=1, source_target_pairs={{0,2},{2,4},{4,6},{6,0},{1,3},{3,5},{5,7},{7,1},{8,10},{10,12},{12... | collective-permute-start | bytes 6152 | tf_op jit(solution)/shard_map/ppermute | solution.py:26
  615.1 11.6 %collective-permute-start.82 = (f32[64,1,128]{2,1,0:T(1,128)S(1)}, f32[64,1,128]{2,1,0:T(1,128)S(1)}, u32[]{:S(2)}, u32[]{:S(2)}) collective-permute-start(f32[64,1,128]{2,1,0:T(1,128)S(1)} %get-tuple-element.64), channel_id=1, source_target_pairs={{8,0},{16,8},{24,16},{9,1},{17,9},{25,17},{10,2},{18,10},{26,18},{... | collective-permute-start | bytes 98312 | tf_op jit(solution)/shard_map/ppermute | solution.py:27
  634.2 78.7 %all-reduce.13.cloned.1.call-start = ((), (), s32[]{:S(2)}) async-start(), calls=%async_computation.6 | async-start | bytes 262144 | tf_op jit(solution)/shard_map/psum | solution.py:16
  668.1 70.0 %all-gather.5.cloned.1.call-start = ((), (), s32[]{:S(2)}) async-start(), calls=%async_computation.3 | async-start | bytes 1572864 | tf_op jit(solution)/shard_map/all_gather | solution.py:125
  (55 other events, 611.4 us)
Sparse Core Ops, SparseCore 0:
  277.3 34.0 all-reduce.10
  314.3 42.0 all-reduce.14
  634.3 33.7 all-reduce.8
  670.8 42.0 all-reduce.12
Sparse Core Ops, SparseCore 1:
  313.4 8.6 all-gather.2
  670.1 8.6 all-gather.4
